TPU v7x, 32 devices: a whole 2x2x4 slice. The times are simulated.
32 devices in a mesh: groups: 2 (over y), seq: 4 (over z), heads: 2 (over x), sub: 2 (over core).
Axes of the slice: x: 2, y: 2, z: 4, core: 2. Of those that a mesh axis runs over, the one named last changes fastest.
Arguments:
- queries: bfloat16 [2048, 8192], P(('groups', 'seq', 'sub'), 'heads'), parts along dimension 0, may hold values from -400 to 400
- keys: bfloat16 [2048, 1024], P(('groups', 'seq', 'sub'), 'heads'), parts along dimension 0, may hold values from -6 to 6
- values: bfloat16 [2048, 1024], P(('groups', 'seq', 'sub'), 'heads'), parts along dimension 0, may hold values from -18 to 18
- half_order: int32 [32], P('groups'), parts along dimension 0, may hold values from 0 to 15, as said below
- frame_lengths: int32 [16], P('groups'), parts along dimension 0, may hold values from 1 to 256, 1024 in all
- out_proj: bfloat16 [8192, 4096], P('heads', ('seq', 'sub')), may hold values from -0.09375 to 0.09375
- residual_in: bfloat16 [2048, 4096], P(('groups', 'seq', 'sub'), 'heads'), parts along dimension 0, may hold values from -40 to 40
- norm_gain: float32 [4096], P('heads'), may hold values from 0.5 to 1.5
Outputs:
- attended: bfloat16 [2048, 8192], P(('groups', 'seq', 'sub'), 'heads'), parts along dimension 0
- hidden_state: bfloat16 [2048, 4096], P(('groups', 'seq', 'sub'), 'heads'), parts along dimension 0
- normed: bfloat16 [2048, 4096], P(('groups', 'seq', 'sub'), 'heads'), parts along dimension 0
There are 2 independent parts, one for each index of `groups`. A program takes and returns all parts, laid end to end along the dimension named above; an argument that names none is the same for every part. Nothing has to cross between parts.
Inputs may be any that keep to these rules, and one draw needn't show every extreme that they name: `half_order`: a permutation of 0 to 15.
All inputs are finite; a program needn't handle non-finite values.
Results may differ from a plain program's by a relative error of at most 0.005.
Values may be sent and summed in bfloat16 or wider, within the bound.
A program may use at most 128 MiB of HBM per device.

v0:
```python
import functools
import math

import jax
import jax.numpy as jnp
from jax import lax
from jax.experimental import pallas as pl
from jax.experimental.pallas import tpu as pltpu
from jax.sharding import PartitionSpec as P

HEAD_WIDTH = 128
MESH = pl.DeviceIdType.MESH


def kernel(dims, order_ref, frames_ref, q_hbm, keys_ref, values_ref, proj_hbm, res_hbm, gain_ref,
           att_out, hidden_out, normed_out,
           kvbuf, attbuf, proj, q_ref, res_ref, bias, pbuf, retbuf, ebuf,
           in_sem, kv_send, kv_recv, at_send, at_recv, ret_send, ret_recv, en_send, en_recv):
    S, C, H, G = dims
    n = S * C
    blocks = n // H
    rows = q_ref.shape[0]
    width = q_ref.shape[1] // G
    cols = proj.shape[1]
    total = n * rows
    z, c, h = lax.axis_index("seq"), lax.axis_index("sub"), lax.axis_index("heads")
    own = z * C + c
    home = own // blocks
    home_slot = own % blocks

    q_copy = pltpu.make_async_copy(q_hbm, q_ref, in_sem.at[0])
    q_copy.start()
    proj_copy = pltpu.make_async_copy(proj_hbm, proj, in_sem.at[1])
    proj_copy.start()
    res_copy = pltpu.make_async_copy(res_hbm, res_ref, in_sem.at[2])
    res_copy.start()

    barrier = pltpu.get_barrier_semaphore()

    def greet(t, carry):
        other = lax.rem(own * H + h + t, n * H)
        place = other // H
        pl.semaphore_signal(
            barrier, inc=1,
            device_id={"seq": place // C, "sub": place % C, "heads": other % H},
            device_id_type=MESH,
        )
        return carry

    lax.fori_loop(1, n * H, greet, 0)

    half_rows = total // order_ref.shape[0]
    per_device = rows // half_rows
    lane = lax.broadcasted_iota(jnp.int32, (1, total), 1)
    key_pos = jnp.zeros((1, total), jnp.int32)
    for t in range(order_ref.shape[0]):
        inside = (lane >= t * half_rows) & (lane < (t + 1) * half_rows)
        key_pos = jnp.where(inside, lane + (order_ref[t] - t) * half_rows, key_pos)
    line = lax.broadcasted_iota(jnp.int32, (rows, 1), 0)
    row_pos = jnp.zeros((rows, 1), jnp.int32)
    for t in range(per_device):
        inside = (line >= t * half_rows) & (line < (t + 1) * half_rows)
        row_pos = jnp.where(inside, line + (order_ref[own * per_device + t] - t) * half_rows, row_pos)
    limit = jnp.zeros((rows, 1), jnp.int32)
    first = jnp.int32(0)
    for f in range(frames_ref.shape[0]):
        limit = limit + jnp.where(first <= row_pos, frames_ref[f], 0)
        first = first + frames_ref[f]
    bias[...] = jnp.where(key_pos < limit, 0.0, -1e30)
    for g in range(G):
        part = slice(g * HEAD_WIDTH, (g + 1) * HEAD_WIDTH)
        kvbuf[own, g, 0] = keys_ref[:, part]
        kvbuf[own, g, 1] = values_ref[:, part]

    pl.semaphore_wait(barrier, n * H - 1)

    def hop(buf, send, recv, side, zs, cs, g):
        target = ({"seq": jnp.minimum(z + 1, S - 1)}, {"seq": jnp.maximum(z - 1, 0)}, {"sub": (c + 1) % C})[side]
        index = zs * C + cs
        return pltpu.make_async_remote_copy(
            src_ref=buf.at[index, g],
            dst_ref=buf.at[index, g],
            send_sem=send.at[side, zs, g],
            recv_sem=recv.at[index, g],
            device_id=target,
            device_id_type=MESH,
        )

    def launch(buf, send, recv, g):
        @pl.when(z + 1 < S)
        def _():
            hop(buf, send, recv, 0, z, c, g).start()

        @pl.when(z > 0)
        def _():
            hop(buf, send, recv, 1, z, c, g).start()

        if C > 1:
            hop(buf, send, recv, 2, z, c, g).start()

    def relay(buf, send, recv, d, g):
        @pl.when(z - d >= 0)
        def _():
            hop(buf, send, recv, 0, z - d, c, g).wait_recv()

            @pl.when(z + 1 < S)
            def _():
                hop(buf, send, recv, 0, z - d, c, g).start()

            if C > 1:
                hop(buf, send, recv, 2, z - d, c, g).start()

        @pl.when(z + d < S)
        def _():
            hop(buf, send, recv, 1, z + d, c, g).wait_recv()

            @pl.when(z > 0)
            def _():
                hop(buf, send, recv, 1, z + d, c, g).start()

            if C > 1:
                hop(buf, send, recv, 2, z + d, c, g).start()

    def from_partner(buf, send, recv, zs, g):
        if C > 1:
            hop(buf, send, recv, 2, zs, (c + 1) % C, g).wait_recv()

    def drain(buf, send, recv, zs, g):
        @pl.when((zs <= z) & (z + 1 < S))
        def _():
            hop(buf, send, recv, 0, zs, c, g).wait_send()

        @pl.when((zs >= z) & (z > 0))
        def _():
            hop(buf, send, recv, 1, zs, c, g).wait_send()

        if C > 1:
            hop(buf, send, recv, 2, zs, c, g).wait_send()

    def kv_relay(g):
        @pl.when(g + 1 < G)
        def _():
            launch(kvbuf, kv_send, kv_recv, g + 1)

        lax.fori_loop(1, S, lambda d, x: (relay(kvbuf, kv_send, kv_recv, d, g), x)[1], 0)

    def kv_partner(g):
        lax.fori_loop(0, S, lambda s, x: (from_partner(kvbuf, kv_send, kv_recv, s, g), x)[1], 0)

    factor = HEAD_WIDTH ** (-0.5) * math.log2(math.e)
    heads_each = width // HEAD_WIDTH
    pack = 2 if heads_each % 2 == 0 else 1
    span = pack * HEAD_WIDTH

    def attention(g):
        kv_partner(g)
        key = kvbuf[:, g, 0].reshape(total, HEAD_WIDTH)
        value = kvbuf[:, g, 1].reshape(total, HEAD_WIDTH)

        def few_heads(b, carry):
            at = pl.multiple_of(g * width + b * span, span)
            q = q_ref[:, pl.ds(at, span)]
            q = jnp.concatenate(
                [q[:, k * HEAD_WIDTH:(k + 1) * HEAD_WIDTH] for k in range(pack)], axis=0
            )
            s = lax.dot_general(q, key, (((1,), (1,)), ((), ())), preferred_element_type=jnp.float32)
            s = (s.reshape(pack, rows, total) + bias[...][None]).reshape(pack * rows, total)
            top = jnp.max(s, axis=-1, keepdims=True)
            w = jnp.exp2((s - top) * factor)
            amount = jnp.sum(w, axis=-1, keepdims=True)
            o = jnp.dot(w.astype(jnp.bfloat16), value, preferred_element_type=jnp.float32)
            o = (o / amount).astype(jnp.bfloat16)
            o = jnp.concatenate([o[k * rows:(k + 1) * rows] for k in range(pack)], axis=1)
            att_out[:, pl.ds(at, span)] = o
            attbuf[own, g, :, pl.ds(pl.multiple_of(b * span, span), span)] = o

            @pl.when((g == 0) & (b + 1 < G))
            def _():
                kv_relay(jnp.minimum(b + 1, G - 1))

            return carry

        lax.fori_loop(0, heads_each // pack, few_heads, 0)

        @pl.when(g == 0)
        def _():
            lax.fori_loop(min(heads_each // pack + 1, G), G, lambda k, x: (kv_relay(k), x)[1], 0)

    def result_copy(index):
        return pltpu.make_async_remote_copy(
            src_ref=pbuf.at[index],
            dst_ref=retbuf.at[h, home_slot],
            send_sem=ret_send.at[index],
            recv_sem=ret_recv.at[h, home_slot],
            device_id={"seq": index // C, "sub": index % C, "heads": home},
            device_id_type=MESH,
        )

    def multiply(zb):
        summed = jnp.zeros((C * rows, cols), jnp.float32)
        for g in range(G):
            from_partner(attbuf, at_send, at_recv, zb, g)
            summed = summed + jnp.dot(
                attbuf[pl.ds(zb * C, C), g].reshape(C * rows, width),
                proj[g * width:(g + 1) * width, :],
                preferred_element_type=jnp.float32,
            )
        summed = summed.astype(jnp.bfloat16)
        for k in range(C):
            index = zb * C + k
            pbuf[index] = summed[k * rows:(k + 1) * rows]
            here = (index == own) & (home == h)

            @pl.when(here)
            def _():
                retbuf[h, home_slot] = summed[k * rows:(k + 1) * rows]

            @pl.when(jnp.logical_not(here))
            def _():
                result_copy(index).start()

    launch(kvbuf, kv_send, kv_recv, 0)
    kv_relay(jnp.int32(0))
    q_copy.wait()

    def head_step(g, carry):
        attention(g)
        launch(attbuf, at_send, at_recv, g)
        return carry

    lax.fori_loop(0, G, head_step, 0)
    proj_copy.wait()
    multiply(z)

    def step(d, carry):
        lax.fori_loop(0, G, lambda g, x: (relay(attbuf, at_send, at_recv, d, g), x)[1], 0)

        @pl.when(z - d >= 0)
        def _():
            multiply(z - d)

        @pl.when(z + d < S)
        def _():
            multiply(z + d)

        return carry

    lax.fori_loop(1, S, step, 0)

    res_copy.wait()
    squares = jnp.zeros((rows, 1), jnp.float32)
    for b in range(blocks):
        where = slice(b * cols, (b + 1) * cols)
        value = res_ref[:, where].astype(jnp.float32)
        for k in range(H):
            @pl.when(jnp.logical_not((home == h) & (home_slot == b) & (k == h)))
            def _():
                pltpu.make_async_remote_copy(
                    src_ref=pbuf.at[0], dst_ref=retbuf.at[k, b],
                    send_sem=ret_send.at[0], recv_sem=ret_recv.at[k, b],
                    device_id={"heads": home}, device_id_type=MESH,
                ).wait_recv()
            value = value + retbuf[k, b].astype(jnp.float32)
        hidden = value.astype(jnp.bfloat16)
        hidden_out[:, where] = hidden
        wide = hidden.astype(jnp.float32)
        squares = squares + jnp.sum(wide * wide, axis=-1, keepdims=True)

    ebuf[h] = jnp.broadcast_to(squares, (rows, 128))

    def share(k, side):
        other = (h + k) % H if side == 0 else (h + H - k) % H
        return pltpu.make_async_remote_copy(
            src_ref=ebuf.at[h], dst_ref=ebuf.at[h if side == 0 else other],
            send_sem=en_send.at[k], recv_sem=en_recv.at[h if side == 0 else other],
            device_id={"heads": (h + k) % H}, device_id_type=MESH,
        )

    for k in range(1, H):
        share(k, 0).start()
    for k in range(1, H):
        share(k, 1).wait_recv()
    energy = ebuf[0]
    for k in range(1, H):
        energy = energy + ebuf[k]
    inverse = lax.rsqrt(energy[:, 0:1] / (H * res_ref.shape[1]) + 1e-06)
    for b in range(blocks):
        where = slice(b * cols, (b + 1) * cols)
        normed_out[:, where] = (
            hidden_out[:, where].astype(jnp.float32) * inverse * gain_ref[:, where]
        ).astype(jnp.bfloat16)

    for k in range(1, H):
        share(k, 0).wait_send()

    def finish(i, carry):
        zs, g = i // G, i % G
        drain(kvbuf, kv_send, kv_recv, zs, g)
        drain(attbuf, at_send, at_recv, zs, g)
        return carry

    lax.fori_loop(0, S * G, finish, 0)

    def finish_results(index, carry):
        @pl.when(jnp.logical_not((index == own) & (home == h)))
        def _():
            result_copy(index).wait_send()
        return carry

    lax.fori_loop(0, n, finish_results, 0)


def shards(dims, queries, keys, values, half_order, frame_lengths, out_proj, residual_in, norm_gain):
    S, C, H = dims
    n = S * C
    rows = queries.shape[0]
    G = keys.shape[1] // HEAD_WIDTH
    width = queries.shape[1] // G
    cols = out_proj.shape[1]
    hbm = pl.BlockSpec(memory_space=pltpu.HBM)
    vmem = pl.BlockSpec(memory_space=pltpu.VMEM)
    smem = pl.BlockSpec(memory_space=pltpu.SMEM)
    dma = pltpu.SemaphoreType.DMA
    bf16, f32 = jnp.bfloat16, jnp.float32
    return pl.pallas_call(
        functools.partial(kernel, (S, C, H, G)),
        out_shape=(
            jax.ShapeDtypeStruct(queries.shape, bf16),
            jax.ShapeDtypeStruct(residual_in.shape, bf16),
            jax.ShapeDtypeStruct(residual_in.shape, bf16),
        ),
        in_specs=[smem, smem, hbm, vmem, vmem, hbm, hbm, vmem],
        out_specs=(vmem, vmem, vmem),
        scratch_shapes=[
            pltpu.VMEM((n, G, 2, rows, HEAD_WIDTH), bf16),
            pltpu.VMEM((n, G, rows, width), bf16),
            pltpu.VMEM(out_proj.shape, bf16),
            pltpu.VMEM(queries.shape, bf16),
            pltpu.VMEM(residual_in.shape, bf16),
            pltpu.VMEM((rows, n * rows), f32),
            pltpu.VMEM((n, rows, cols), bf16),
            pltpu.VMEM((H, n // H, rows, cols), bf16),
            pltpu.VMEM((H, rows, 128), f32),
            dma((3,)),
            dma((3, S, G)),
            dma((n, G)),
            dma((3, S, G)),
            dma((n, G)),
            dma((n,)),
            dma((H, n // H)),
            dma((H,)),
            dma((H,)),
        ],
        compiler_params=pltpu.CompilerParams(
            collective_id=0, has_side_effects=True, vmem_limit_bytes=51 * 1024 * 1024
        ),
    )(half_order, frame_lengths, queries, keys, values, out_proj, residual_in, norm_gain[None, :])


def solution(mesh):
    dims = (mesh.shape["seq"], mesh.shape["sub"], mesh.shape["heads"])
    token = P(("groups", "seq", "sub"), "heads")
    in_specs = (
        token, token, token, P("groups"), P("groups"),
        P("heads", ("seq", "sub")), token, P("heads"),
    )
    return jax.shard_map(
        functools.partial(shards, dims), mesh=mesh, in_specs=in_specs,
        out_specs=(token, token, token), check_vma=False,
    )
```

profile of v0, /device:TPU:0, one launch (start us, length us, event | category | flops | bytes accessed | tf_op | source)
XLA Modules:
  0.0 132.4 jit_solution(2300080142788512269)
XLA Ops:
  0.6 0.0 copy-start
  0.6 1.0 copy-done
  1.7 0.0 copy-start.1
  1.7 0.9 copy-done.1
  2.6 0.0 copy-start.2
  2.6 0.9 copy-done.2
  3.5 0.0 copy-start.3
  3.5 0.7 copy-done.3
  4.2 0.0 copy-start.4
  4.2 0.7 copy-done.4
  4.8 0.0 copy-start.5
  4.8 0.7 copy-done.5
  5.5 124.3 %shard_map.103 = (bf16[128,4096]{1,0:T(8,128)(2,1)S(1)}, bf16[128,2048]{1,0:T(8,128)(2,1)S(1)}, bf16[128,2048]{1,0:T(8,128)(2,1)S(1)}) custom-call(s32[16]{0:T(128)S(1)} %copy-done.4, s32[8]{0:T(128)S(1)} %copy-done.5, bf16[128,4096]{1,0:T(8,128)(2,1)} %q_hbm.1, bf16[128,512]{1,0:T(8,128)(2,1)S(1)} %copy-done.1, bf16[128,512]{1,0:T(8,128)(2,1)S(1)} %copy-done.2, ...), custom_call_target="tpu_custom_call" | custom-call | tf_op jit(solution)/shard_map/pallas_call | solution.py:325
  129.8 1.0 copy.14
  130.8 0.8 copy.15
  131.6 0.8 copy.16
Async XLA Ops:
  0.6 1.0 copy-start
  1.7 0.9 copy-start.1
  2.6 0.9 copy-start.2
  3.5 0.7 copy-start.3
  4.2 0.7 copy-start.4
  4.8 0.7 copy-start.5
where the time goes:
time: 134 us; the launch traced here: 132 us
  Pallas kernels  124 us (93%)
  local copies, waits for them, and re-layouts  7.41 us (6%)
    pallas_call x1, Pallas kernels, shards(): pl.pallas_call(functools.partial(kernel, (S, C, H, G)), out_shape=(jax.Sh...  124 us
    unnamed x15, local copies, waits for them, and re-layouts  7.41 us

commit v1 on v0

v1 whole, which is shorter than its diff:
```python
import functools
import math

import jax
import jax.numpy as jnp
from jax import lax
from jax.experimental import pallas as pl
from jax.experimental.pallas import tpu as pltpu
from jax.sharding import PartitionSpec as P

HEAD_WIDTH = 128
MESH = pl.DeviceIdType.MESH


def loop(low, high, body):
    def step(i, carry):
        body(i)
        return carry

    lax.fori_loop(low, high, step, 0)


def kernel(dims, order_ref, frames_ref, q_hbm, k_hbm, v_hbm, proj_hbm, res_hbm, gain_hbm,
           att_out, hidden_out, normed_out,
           kvbuf, attbuf, wall, wext, q_ref, res_ref, gain_ref, bias, pbuf, xbuf, obuf, mbuf, retbuf, ebuf,
           in_sem, kv_in, kv_send, kv_recv, at_send, at_recv, x_send, x_recv, ret_send, ret_recv, m_recv,
           w_send, w_recv, wf_send, en_send, en_recv):
    S, C, H, G, Y, Q, NJ, hub, near = dims
    n = S * C
    blocks = n // H
    rows = q_ref.shape[0]
    width = q_ref.shape[1] // G
    deep, thin = wall.shape[1], wall.shape[2]
    total = n * rows
    part_rows = wext.shape[1] // Y
    piece_rows = part_rows // NJ
    pieces = Q * NJ
    steps = width // HEAD_WIDTH
    pack = 2 if steps % 2 == 0 else 1
    steps = steps // pack
    span = pack * HEAD_WIDTH
    pace, lead = min(3, steps), min(1, steps - 1)
    side_lag = min(2, G - 1)
    y, z = lax.axis_index("groups"), lax.axis_index("seq")
    c, h = lax.axis_index("sub"), lax.axis_index("heads")
    own = z * C + c
    inner = (z >= 1) & (z <= S - 2) if hub else (z >= 0)
    outer = jnp.logical_not(inner)
    is_hub = (z == 1) | (z == S - 2)
    edge = jnp.where(z < S // 2, 0, S - 1)
    hub_of_edge = jnp.where(z < S // 2, 1, S - 2)
    inward = jnp.where(z < S // 2, 1, -1)

    def reach(g):
        if not hub:
            return 0, S - 1
        return jnp.where(g < near, 0, 1), jnp.where(g < near, S - 1, S - 2)

    barrier = pltpu.get_barrier_semaphore()

    def greet(t):
        other = lax.rem(own * H + h + t, n * H)
        place = other // H
        pl.semaphore_signal(
            barrier, inc=1,
            device_id={"seq": place // C, "sub": place % C, "heads": other % H},
            device_id_type=MESH,
        )

    loop(1, n * H, greet)
    greeted = n * H - 1
    if hub:
        for k in range(1, Y):
            pl.semaphore_signal(barrier, inc=1, device_id={"groups": (y + k) % Y}, device_id_type=MESH)
        greeted += Y - 1

    kv_copies = []
    for g in range(G):
        part = slice(g * HEAD_WIDTH, (g + 1) * HEAD_WIDTH)
        kv_copies.append(pltpu.make_async_copy(k_hbm.at[:, part], kvbuf.at[own, g, 0], kv_in.at[g, 0]))
        kv_copies.append(pltpu.make_async_copy(v_hbm.at[:, part], kvbuf.at[own, g, 1], kv_in.at[g, 1]))
    for copy in kv_copies:
        copy.start()
    q_copy = pltpu.make_async_copy(q_hbm, q_ref, in_sem.at[0])
    q_copy.start()
    res_copy = pltpu.make_async_copy(res_hbm, res_ref, in_sem.at[1])
    res_copy.start()
    gain_copy = pltpu.make_async_copy(gain_hbm, gain_ref, in_sem.at[2])
    gain_copy.start()

    def own_weights(q, depth):
        return pltpu.make_async_copy(
            proj_hbm.at[:depth, q * thin:(q + 1) * thin], wall.at[q, :depth, :], in_sem.at[3 + q]
        )

    def each_own_weights(act):
        @pl.when(inner)
        def _():
            for q in range(Q):
                act(own_weights(q, deep))

        if hub and near:
            @pl.when(outer)
            def _():
                for q in range(Q):
                    act(own_weights(q, near * width))

    each_own_weights(lambda copy: copy.start())
    for copy in kv_copies:
        copy.wait()
    with jax.named_scope("barrier"):
        pl.semaphore_wait(barrier, greeted)

    def hop(buf, send, recv, side, zs, cs, g, cut=None):
        target = ({"seq": jnp.minimum(z + 1, S - 1)}, {"seq": jnp.maximum(z - 1, 0)}, {"sub": (c + 1) % C})[side]
        index = zs * C + cs
        block = buf.at[index, g] if cut is None else buf.at[index, g, :, cut]
        return pltpu.make_async_remote_copy(
            src_ref=block,
            dst_ref=block,
            send_sem=send.at[side, zs, g],
            recv_sem=recv.at[index, g],
            device_id=target,
            device_id_type=MESH,
        )

    def launch(buf, send, recv, g, lo, hi, cut=None):
        @pl.when(z + 1 <= hi)
        def _():
            hop(buf, send, recv, 0, z, c, g, cut).start()

        @pl.when(z - 1 >= lo)
        def _():
            hop(buf, send, recv, 1, z, c, g, cut).start()

        if C > 1:
            @pl.when((z >= lo) & (z <= hi))
            def _():
                hop(buf, send, recv, 2, z, c, g, cut).start()

    def relay_right(buf, send, recv, d, g, lo, hi):
        @pl.when((z - d >= 0) & (z >= lo) & (z <= hi))
        def _():
            hop(buf, send, recv, 0, z - d, c, g).wait_recv()

            @pl.when(z + 1 <= hi)
            def _():
                hop(buf, send, recv, 0, z - d, c, g).start()

            if C > 1:
                hop(buf, send, recv, 2, z - d, c, g).start()

    def relay_left(buf, send, recv, d, g, lo, hi):
        @pl.when((z + d < S) & (z >= lo) & (z <= hi))
        def _():
            hop(buf, send, recv, 1, z + d, c, g).wait_recv()

            @pl.when(z - 1 >= lo)
            def _():
                hop(buf, send, recv, 1, z + d, c, g).start()

            if C > 1:
                hop(buf, send, recv, 2, z + d, c, g).start()

    def from_partner(buf, send, recv, zs, g):
        if C > 1:
            hop(buf, send, recv, 2, zs, (c + 1) % C, g).wait_recv()

    def drain(buf, send, recv, zs, g, lo, hi):
        @pl.when((zs <= z) & (z + 1 <= hi))
        def _():
            hop(buf, send, recv, 0, zs, c, g).wait_send()

        @pl.when((zs >= z) & (z - 1 >= lo))
        def _():
            hop(buf, send, recv, 1, zs, c, g).wait_send()

        if C > 1:
            @pl.when((z >= lo) & (z <= hi))
            def _():
                hop(buf, send, recv, 2, zs, c, g).wait_send()

    def w_block(i, side):
        q, j = i // NJ, i % NJ
        return q, side * part_rows + j * piece_rows

    def w_out(i):
        q, at = w_block(i, y)
        return pltpu.make_async_remote_copy(
            src_ref=proj_hbm.at[
                pl.ds(pl.multiple_of(near * width + at, piece_rows), piece_rows),
                pl.ds(pl.multiple_of(q * thin, thin), thin),
            ],
            dst_ref=wext.at[q, pl.ds(pl.multiple_of(at, piece_rows), piece_rows), :],
            send_sem=w_send.at[i], recv_sem=w_recv.at[y, i],
            device_id={"seq": hub_of_edge}, device_id_type=MESH,
        )

    def w_pass(i, k, side):
        q, at = w_block(i, side)
        block = wext.at[q, pl.ds(pl.multiple_of(at, piece_rows), piece_rows), :]
        return pltpu.make_async_remote_copy(
            src_ref=block, dst_ref=block,
            send_sem=wf_send.at[k - 1, i], recv_sem=w_recv.at[side, i],
            device_id={"groups": (y + k) % Y}, device_id_type=MESH,
        )

    def w_relay(i):
        with jax.named_scope("wwait"):
            w_pass(i, 1, y).wait_recv()
        for k in range(1, Y):
            w_pass(i, k, y).start()

    def wave(s):
        @pl.when((s + 2 < G) & (inner if hub else True))
        def _():
            launch(kvbuf, kv_send, kv_recv, jnp.minimum(s + 2, G - 1), 0, S - 1)

        def one(d):
            g = s + 1 - d

            @pl.when((g >= 0) & (g < G))
            def _():
                at = jnp.clip(g, 0, G - 1)
                relay_right(kvbuf, kv_send, kv_recv, d, at, 0, S - 1)
                relay_left(kvbuf, kv_send, kv_recv, d, at, 0, S - 1)

        with jax.named_scope("wave"):
            loop(1, S, one)

    def kv_partner(g):
        with jax.named_scope("kvpartner"):
            loop(0, S, lambda s: from_partner(kvbuf, kv_send, kv_recv, s, g))

    loop(0, min(2, G), lambda g: launch(kvbuf, kv_send, kv_recv, g, 0, S - 1))
    if hub:
        @pl.when(outer)
        def _():
            loop(min(2, G), G, lambda g: launch(kvbuf, kv_send, kv_recv, g, 0, S - 1))
            loop(0, pieces, lambda i: w_out(i).start())

    half_rows = total // order_ref.shape[0]
    per_device = rows // half_rows
    lane = lax.broadcasted_iota(jnp.int32, (1, total), 1)
    key_pos = jnp.zeros((1, total), jnp.int32)
    for t in range(order_ref.shape[0]):
        inside = (lane >= t * half_rows) & (lane < (t + 1) * half_rows)
        key_pos = jnp.where(inside, lane + (order_ref[t] - t) * half_rows, key_pos)
    line = lax.broadcasted_iota(jnp.int32, (rows, 1), 0)
    row_pos = jnp.zeros((rows, 1), jnp.int32)
    for t in range(per_device):
        inside = (line >= t * half_rows) & (line < (t + 1) * half_rows)
        row_pos = jnp.where(inside, line + (order_ref[own * per_device + t] - t) * half_rows, row_pos)
    limit = jnp.zeros((rows, 1), jnp.int32)
    first = jnp.int32(0)
    for f in range(frames_ref.shape[0]):
        limit = limit + jnp.where(first <= row_pos, frames_ref[f], 0)
        first = first + frames_ref[f]
    bias[...] = jnp.where(key_pos < limit, 0.0, -1e30)

    factor = HEAD_WIDTH ** (-0.5) * math.log2(math.e)

    def attention(g):
        kv_partner(g)
        key = kvbuf[:, g, 0].reshape(total, HEAD_WIDTH)
        value = kvbuf[:, g, 1].reshape(total, HEAD_WIDTH)

        def few_heads(b):
            at = pl.multiple_of(g * width + b * span, span)
            q = q_ref[:, pl.ds(at, span)]
            q = jnp.concatenate(
                [q[:, k * HEAD_WIDTH:(k + 1) * HEAD_WIDTH] for k in range(pack)], axis=0
            )
            s = lax.dot_general(q, key, (((1,), (1,)), ((), ())), preferred_element_type=jnp.float32)
            s = (s.reshape(pack, rows, total) + bias[...][None]).reshape(pack * rows, total)
            top = jnp.max(s, axis=-1, keepdims=True)
            w = jnp.exp2((s - top) * factor)
            amount = jnp.sum(w, axis=-1, keepdims=True)
            o = jnp.dot(w.astype(jnp.bfloat16), value, preferred_element_type=jnp.float32)
            o = (o / amount).astype(jnp.bfloat16)
            o = jnp.concatenate([o[k * rows:(k + 1) * rows] for k in range(pack)], axis=1)
            att_out[:, pl.ds(at, span)] = o
            cut = pl.ds(pl.multiple_of(b * span, span), span)
            attbuf[own, g, :, cut] = o
            launch(attbuf, at_send, at_recv, g, *reach(g), cut)

            turn = g * steps + b - lead

            @pl.when((turn >= 0) & (turn % pace == 0) & (turn // pace < G - 1))
            def _():
                wave(S - 1 + turn // pace)

        loop(0, steps, few_heads)

    def x_copy(t, u):
        return pltpu.make_async_remote_copy(
            src_ref=pbuf.at[u, t],
            dst_ref=xbuf.at[u, t // H, h],
            send_sem=x_send.at[u, t],
            recv_sem=x_recv.at[u, t // H, h],
            device_id={"heads": t % H},
            device_id_type=MESH,
        )

    def multiply(zb, u, weights, g0, g1):
        summed = jnp.zeros((C * rows, thin), jnp.float32)
        for g in range(g0, g1):
            summed = summed + jnp.dot(
                attbuf[pl.ds(zb * C, C), g].reshape(C * rows, width),
                weights[u % Q, (g - g0) * width:(g - g0 + 1) * width, :],
                preferred_element_type=jnp.float32,
            )
        summed = summed.astype(jnp.bfloat16)
        for k in range(C):
            t = zb * C + k
            mine = t % H == h

            @pl.when(mine)
            def _():
                xbuf[u, t // H, h] = summed[k * rows:(k + 1) * rows]

            @pl.when(jnp.logical_not(mine))
            def _():
                pbuf[u, t] = summed[k * rows:(k + 1) * rows]
                x_copy(t, u).start()

    def place_of(u):
        block = jnp.where(u < Q, own, edge * C + c)
        return block // blocks, block % blocks, u % Q

    def result_copy(t, u):
        home, slot, q = place_of(u)
        return pltpu.make_async_remote_copy(
            src_ref=obuf.at[u, t // H],
            dst_ref=retbuf.at[slot, q],
            send_sem=ret_send.at[u, t // H],
            recv_sem=ret_recv.at[slot, q],
            device_id={"seq": t // C, "sub": t % C, "heads": home},
            device_id_type=MESH,
        )

    def merge_copy(t, u):
        return pltpu.make_async_remote_copy(
            src_ref=obuf.at[u, t // H],
            dst_ref=mbuf.at[u % Q, t // H],
            send_sem=ret_send.at[u, t // H],
            recv_sem=m_recv.at[u % Q, t // H],
            device_id={"seq": hub_of_edge},
            device_id_type=MESH,
        )

    def reduce(zb, u):
        home, slot, q = place_of(u)
        for k in range(C):
            t = zb * C + k

            @pl.when(t % H == h)
            def _():
                value = jnp.zeros((rows, thin), jnp.float32)
                for other in range(H):
                    @pl.when(other != h)
                    def _():
                        pltpu.make_async_remote_copy(
                            src_ref=pbuf.at[u, t], dst_ref=xbuf.at[u, t // H, other],
                            send_sem=x_send.at[u, t], recv_sem=x_recv.at[u, t // H, other],
                            device_id={"heads": (h + 1) % H}, device_id_type=MESH,
                        ).wait_recv()
                    value = value + xbuf[u, t // H, other].astype(jnp.float32)
                obuf[u, t // H] = value.astype(jnp.bfloat16)
                if hub and near:
                    @pl.when(u >= Q)
                    def _():
                        merge_copy(t, u).wait_recv()
                        obuf[u, t // H] = (value + mbuf[q, t // H].astype(jnp.float32)).astype(jnp.bfloat16)

                    @pl.when(outer)
                    def _():
                        merge_copy(t, u).start()
                here = (t == own) & (home == h)

                @pl.when(inner & here)
                def _():
                    retbuf[slot, q] = obuf[u, t // H]

                @pl.when(inner & jnp.logical_not(here))
                def _():
                    result_copy(t, u).start()

    def multiply_all(zb):
        @pl.when(inner)
        def _():
            with jax.named_scope("arrive"):
                loop(0, G, lambda g: from_partner(attbuf, at_send, at_recv, zb, g))
            with jax.named_scope("mult"):
                loop(0, Q, lambda u: multiply(zb, u, wall, 0, G))

        if hub and near:
            @pl.when(outer)
            def _():
                with jax.named_scope("arrive"):
                    loop(0, near, lambda g: from_partner(attbuf, at_send, at_recv, zb, g))
                with jax.named_scope("multend"):
                    loop(0, Q, lambda u: multiply(zb, u, wall, 0, near))

    def multiply_extra(zb):
        @pl.when(is_hub)
        def _():
            with jax.named_scope("extra"):
                loop(Q, 2 * Q, lambda u: multiply(zb, u, wext, near, G))

    def reduce_extra(zb):
        @pl.when(is_hub)
        def _():
            with jax.named_scope("reduceextra"):
                loop(Q, 2 * Q, lambda u: reduce(zb, u))

    def reduce_all(zb):
        with jax.named_scope("reduce"):
            @pl.when((inner | outer) if near else inner)
            def _():
                loop(0, Q, lambda u: reduce(zb, u))

    def by_slot(k, act, self_slot):
        def pick(which):
            since = jnp.where(which == 2, k - side_lag, k)
            d = jnp.where(which == 0, 0, since // G + 1)
            zb = z + jnp.where(which == 2, -inward, inward) * d
            due = jnp.where(which == 0, k == self_slot, (since >= 0) & (since % G == G - 1))

            @pl.when(due & (zb >= 0) & (zb < S))
            def _():
                act(jnp.clip(zb, 0, S - 1))

        loop(0, 3, pick)

    def relay_slot(k, rightward):
        d, g = k // G + 1, k % G
        move = relay_right if rightward else relay_left
        move(attbuf, at_send, at_recv, d, g, *reach(g))

    loop(0, S - 1, wave)
    q_copy.wait()

    def head_step(g):
        with jax.named_scope("attention"):
            attention(g)
        if hub:
            for k in range(2):
                @pl.when(is_hub & (g > 0) & ((g - 1) * 2 + k < pieces))
                def _():
                    w_relay((g - 1) * 2 + k)

    loop(0, G, head_step)
    each_own_weights(lambda copy: copy.wait())

    def slot_step(k):
        if hub:
            @pl.when(is_hub & (k == min(1, side_lag)))
            def _():
                loop(min(pieces, 2 * (G - 1)), pieces, w_relay)

        with jax.named_scope("arelay"):
            for rightward in (False, True):
                inner_side = (inward < 0) if rightward else (inward > 0)
                at = jnp.where(inner_side, k, k - side_lag)

                @pl.when(at >= 0)
                def _():
                    relay_slot(jnp.maximum(at, 0), rightward)

        if hub:
            @pl.when(is_hub & (k == side_lag))
            def _():
                with jax.named_scope("wother"):
                    for t in range(1, Y):
                        loop(0, pieces, lambda i: w_pass(i, 1, (y + t) % Y).wait_recv())

        by_slot(k, multiply_all, 0)
        if hub:
            by_slot(k, multiply_extra, side_lag)

        @pl.when(k > 0)
        def _():
            by_slot(k - 1, reduce_all, 0)

    slots = (S - 1) * G + side_lag
    loop(0, slots, slot_step)
    by_slot(slots - 1, reduce_all, 0)
    if hub:
        loop(0, slots, lambda k: by_slot(k, reduce_extra, side_lag))

    res_copy.wait()
    squares = jnp.zeros((rows, 1), jnp.float32)
    for b in range(blocks):
        block = h * blocks + b
        source = block // C
        if hub:
            source = jnp.clip(source, 1, S - 2)
        made_here = (source == z) & (block % C == c) & (own % H == h)
        for q in range(Q):
            @pl.when(jnp.logical_not(made_here))
            def _():
                with jax.named_scope(f"final{b}_{q}"):
                    pltpu.make_async_remote_copy(
                        src_ref=obuf.at[0, 0], dst_ref=retbuf.at[b, q],
                        send_sem=ret_send.at[0, 0], recv_sem=ret_recv.at[b, q],
                        device_id={"heads": (h + 1) % H}, device_id_type=MESH,
                    ).wait_recv()
            where = slice((b * Q + q) * thin, (b * Q + q + 1) * thin)
            hidden = (res_ref[:, where].astype(jnp.float32) + retbuf[b, q].astype(jnp.float32)).astype(jnp.bfloat16)
            hidden_out[:, where] = hidden
            wide = hidden.astype(jnp.float32)
            squares = squares + jnp.sum(wide * wide, axis=-1, keepdims=True)

    ebuf[h] = jnp.broadcast_to(squares, (rows, 128))

    def share(k, side):
        other = (h + k) % H if side == 0 else (h + H - k) % H
        return pltpu.make_async_remote_copy(
            src_ref=ebuf.at[h], dst_ref=ebuf.at[h if side == 0 else other],
            send_sem=en_send.at[k], recv_sem=en_recv.at[h if side == 0 else other],
            device_id={"heads": (h + k) % H}, device_id_type=MESH,
        )

    for k in range(1, H):
        share(k, 0).start()
    with jax.named_scope("energy"):
        for k in range(1, H):
            share(k, 1).wait_recv()
    energy = ebuf[0]
    for k in range(1, H):
        energy = energy + ebuf[k]
    inverse = lax.rsqrt(energy[:, 0:1] / (H * res_ref.shape[1]) + 1e-06)
    gain_copy.wait()
    for b in range(blocks):
        where = slice(b * Q * thin, (b + 1) * Q * thin)
        normed_out[:, where] = (
            hidden_out[:, where].astype(jnp.float32) * inverse * gain_ref[:, where]
        ).astype(jnp.bfloat16)

    for k in range(1, H):
        share(k, 0).wait_send()

    def finish(i):
        zs, g = i // G, i % G
        drain(kvbuf, kv_send, kv_recv, zs, g, 0, S - 1)
        drain(attbuf, at_send, at_recv, zs, g, *reach(g))

    with jax.named_scope("drain"):
        loop(0, S * G, finish)

    def finish_results(u):
        home, slot, q = place_of(u)

        def finish_one(t):
            @pl.when(t % H != h)
            def _():
                x_copy(t, u).wait_send()

            @pl.when(inner & (t % H == h) & jnp.logical_not((t == own) & (home == h)))
            def _():
                result_copy(t, u).wait_send()

            if hub and near:
                @pl.when(outer & (t % H == h))
                def _():
                    merge_copy(t, u).wait_send()

        @pl.when(((u < Q) & ((inner | outer) if near else inner)) | ((u >= Q) & is_hub))
        def _():
            loop(0, n, finish_one)

    loop(0, Q * (2 if hub else 1), finish_results)

    if hub:
        @pl.when(outer)
        def _():
            loop(0, pieces, lambda i: w_out(i).wait_send())

        @pl.when(is_hub)
        def _():
            for k in range(1, Y):
                loop(0, pieces, lambda i: w_pass(i, k, y).wait_send())


def shards(dims, queries, keys, values, half_order, frame_lengths, out_proj, residual_in, norm_gain):
    S, C, H, Y = dims
    n = S * C
    rows = queries.shape[0]
    G = keys.shape[1] // HEAD_WIDTH
    width = queries.shape[1] // G
    deep, cols = out_proj.shape
    hub = S >= 4
    Q = 2 if cols % 512 == 0 else 1
    NJ = 4
    near = G // 2
    thin = cols // Q
    U = Q * (2 if hub else 1)
    hbm = pl.BlockSpec(memory_space=pltpu.HBM)
    vmem = pl.BlockSpec(memory_space=pltpu.VMEM)
    smem = pl.BlockSpec(memory_space=pltpu.SMEM)
    dma = pltpu.SemaphoreType.DMA
    bf16, f32 = jnp.bfloat16, jnp.float32
    return pl.pallas_call(
        functools.partial(kernel, (S, C, H, G, Y, Q, NJ, hub, near)),
        out_shape=(
            jax.ShapeDtypeStruct(queries.shape, bf16),
            jax.ShapeDtypeStruct(residual_in.shape, bf16),
            jax.ShapeDtypeStruct(residual_in.shape, bf16),
        ),
        in_specs=[smem, smem, hbm, hbm, hbm, hbm, hbm, hbm],
        out_specs=(vmem, vmem, vmem),
        scratch_shapes=[
            pltpu.VMEM((n, G, 2, rows, HEAD_WIDTH), bf16),
            pltpu.VMEM((n, G, rows, width), bf16),
            pltpu.VMEM((Q, deep, thin), bf16),
            pltpu.VMEM((Q, (G - near) * width, thin), bf16),
            pltpu.VMEM(queries.shape, bf16),
            pltpu.VMEM(residual_in.shape, bf16),
            pltpu.VMEM((1, norm_gain.shape[0]), f32),
            pltpu.VMEM((rows, n * rows), f32),
            pltpu.VMEM((U, n, rows, thin), bf16),
            pltpu.VMEM((U, n // H, H, rows, thin), bf16),
            pltpu.VMEM((U, n // H, rows, thin), bf16),
            pltpu.VMEM((Q, n // H, rows, thin), bf16),
            pltpu.VMEM((n // H, Q, rows, thin), bf16),
            pltpu.VMEM((H, rows, 128), f32),
            dma((3 + Q,)),
            dma((G, 2)),
            dma((3, S, G)),
            dma((n, G)),
            dma((3, S, G)),
            dma((n, G)),
            dma((U, n)),
            dma((U, n // H, H)),
            dma((U, n // H)),
            dma((n // H, Q)),
            dma((Q, n // H)),
            dma((Q * NJ,)),
            dma((Y, Q * NJ)),
            dma((max(Y - 1, 1), Q * NJ)),
            dma((H,)),
            dma((H,)),
        ],
        compiler_params=pltpu.CompilerParams(
            collective_id=0, has_side_effects=True, vmem_limit_bytes=51 * 1024 * 1024
        ),
    )(half_order, frame_lengths, queries, keys, values, out_proj, residual_in, norm_gain[None, :])


def solution(mesh):
    dims = (mesh.shape["seq"], mesh.shape["sub"], mesh.shape["heads"], mesh.shape["groups"])
    token = P(("groups", "seq", "sub"), "heads")
    in_specs = (
        token, token, token, P("groups"), P("groups"),
        P("heads", ("seq", "sub")), token, P("heads"),
    )
    return jax.shard_map(
        functools.partial(shards, dims), mesh=mesh, in_specs=in_specs,
        out_specs=(token, token, token), check_vma=False,
    )
```

time: 134 us -> 103 us (0.77); the launches traced: 132 us -> 103 us
  Pallas kernels: 124 us -> 95.1 us
    pallas_call x1, Pallas kernels: 124 us -> 95.1 us  [shards(): pl.pallas_call(functools.partial(kernel, (S, C, H, G, Y, Q, NJ, hub, near...]
where the time goes in v1:
time: 103 us
  Pallas kernels  95.1 us (92%)
  local copies, waits for them, and re-layouts  7.41 us (7%)
    pallas_call x1, Pallas kernels, shards(): pl.pallas_call(functools.partial(kernel, (S, C, H, G, Y, Q, NJ, hub, near...  95.1 us
    unnamed x15, local copies, waits for them, and re-layouts  7.41 us

profile of v1, /device:TPU:0, one launch (start us, length us, event | category | flops | bytes accessed | tf_op | source)
XLA Modules:
  0.0 103.1 jit_solution(3534825089702708913)
XLA Ops:
  0.6 0.0 copy-start
  0.6 1.0 %copy-done = bf16[128,2048]{1,0:T(8,128)(2,1)S(1)} copy-done((bf16[128,2048]{1,0:T(8,128)(2,1)S(1)}, bf16[128,2048]{1,0:T(8,128)(2,1)}, u32[]{:S(2)}) %copy-start) | copy-done | bytes 524312
  1.7 0.0 copy-start.1
  1.7 0.9 copy-done.1
  2.6 0.0 copy-start.2
  2.6 0.9 copy-done.2
  3.5 0.0 copy-start.3
  3.5 0.7 copy-done.3
  4.2 0.0 copy-start.4
  4.2 0.7 copy-done.4
  4.8 0.0 copy-start.5
  4.8 0.7 copy-done.5
  5.5 95.1 %shard_map.103 = (bf16[128,4096]{1,0:T(8,128)(2,1)S(1)}, bf16[128,2048]{1,0:T(8,128)(2,1)S(1)}, bf16[128,2048]{1,0:T(8,128)(2,1)S(1)}) custom-call(s32[16]{0:T(128)S(1)} %copy-done.4, s32[8]{0:T(128)S(1)} %copy-done.5, bf16[128,4096]{1,0:T(8,128)(2,1)} %q_hbm.1, bf16[128,512]{1,0:T(8,128)(2,1)S(1)} %copy-done.1, bf16[128,512]{1,0:T(8,128)(2,1)S(1)} %copy-done.2, ...), custom_call_target="tpu_custom_call" | custom-call | tf_op jit(solution)/shard_map/pallas_call | solution.py:604
  100.6 1.0 copy.14
  101.6 0.8 copy.15
  102.3 0.8 copy.16
Async XLA Ops:
  0.6 1.0 %copy-start = (bf16[128,2048]{1,0:T(8,128)(2,1)S(1)}, bf16[128,2048]{1,0:T(8,128)(2,1)}, u32[]{:S(2)}) copy-start(bf16[128,2048]{1,0:T(8,128)(2,1)} %res_hbm.1) | copy-start | bytes 1572868
  1.7 0.9 copy-start.1
  2.6 0.9 copy-start.2
  3.5 0.7 copy-start.3
  4.2 0.7 copy-start.4
  4.8 0.7 copy-start.5

commit v2 on v1

--- a/solution.py
+++ b/solution.py
@@ -20,10 +20,10 @@
     lax.fori_loop(low, high, step, 0)
 
 
-def kernel(dims, order_ref, frames_ref, q_hbm, k_hbm, v_hbm, proj_hbm, res_hbm, gain_hbm,
-           att_out, hidden_out, normed_out,
-           kvbuf, attbuf, wall, wext, q_ref, res_ref, gain_ref, bias, pbuf, xbuf, obuf, mbuf, retbuf, ebuf,
-           in_sem, kv_in, kv_send, kv_recv, at_send, at_recv, x_send, x_recv, ret_send, ret_recv, m_recv,
+def kernel(dims, order_hbm, frames_hbm, q_hbm, k_hbm, v_hbm, proj_hbm, res_hbm, gain_hbm,
+           att_hbm, hidden_hbm, normed_hbm,
+           order_ref, frames_ref, hidden_out, normed_out, acc, kvbuf, attbuf, wall, wext, q_ref, res_ref, gain_ref, bias, pbuf, xbuf, obuf, mbuf, retbuf, ebuf,
+           in_sem, out_sem, kv_in, kv_send, kv_recv, at_send, at_recv, x_send, x_recv, ret_send, ret_recv, m_recv,
            w_send, w_recv, wf_send, en_send, en_recv):
     S, C, H, G, Y, Q, NJ, hub, near = dims
     n = S * C
@@ -40,7 +40,12 @@
     steps = steps // pack
     span = pack * HEAD_WIDTH
     pace, lead = min(3, steps), min(1, steps - 1)
-    side_lag = min(2, G - 1)
+    R = 2 if steps % 2 == 0 else 1
+    E = G * R
+    cut_width = width // R
+    side_lag = E // 2
+    self_done = E // 2
+    extra_slot = min(side_lag + 2, E - 1)
     y, z = lax.axis_index("groups"), lax.axis_index("seq")
     c, h = lax.axis_index("sub"), lax.axis_index("heads")
     own = z * C + c
@@ -54,8 +59,23 @@
     def reach(g):
         if not hub:
             return 0, S - 1
-        return jnp.where(g < near, 0, 1), jnp.where(g < near, S - 1, S - 2)
-
+        return jnp.where(g < near * R, 0, 1), jnp.where(g < near * R, S - 1, S - 2)
+
+    kv_copies = []
+    for g in range(G):
+        part = slice(g * HEAD_WIDTH, (g + 1) * HEAD_WIDTH)
+        kv_copies.append(pltpu.make_async_copy(k_hbm.at[:, part], kvbuf.at[own, g, 0], kv_in.at[g, 0]))
+        kv_copies.append(pltpu.make_async_copy(v_hbm.at[:, part], kvbuf.at[own, g, 1], kv_in.at[g, 1]))
+    for copy in kv_copies:
+        copy.start()
+    table_copies = [
+        pltpu.make_async_copy(order_hbm, order_ref, in_sem.at[3]),
+        pltpu.make_async_copy(frames_hbm, frames_ref, in_sem.at[4]),
+    ]
+    for copy in table_copies:
+        copy.start()
+    q_copy = pltpu.make_async_copy(q_hbm, q_ref, in_sem.at[0])
+    q_copy.start()
     barrier = pltpu.get_barrier_semaphore()
 
     def greet(t):
@@ -74,15 +94,6 @@
             pl.semaphore_signal(barrier, inc=1, device_id={"groups": (y + k) % Y}, device_id_type=MESH)
         greeted += Y - 1
 
-    kv_copies = []
-    for g in range(G):
-        part = slice(g * HEAD_WIDTH, (g + 1) * HEAD_WIDTH)
-        kv_copies.append(pltpu.make_async_copy(k_hbm.at[:, part], kvbuf.at[own, g, 0], kv_in.at[g, 0]))
-        kv_copies.append(pltpu.make_async_copy(v_hbm.at[:, part], kvbuf.at[own, g, 1], kv_in.at[g, 1]))
-    for copy in kv_copies:
-        copy.start()
-    q_copy = pltpu.make_async_copy(q_hbm, q_ref, in_sem.at[0])
-    q_copy.start()
     res_copy = pltpu.make_async_copy(res_hbm, res_ref, in_sem.at[1])
     res_copy.start()
     gain_copy = pltpu.make_async_copy(gain_hbm, gain_ref, in_sem.at[2])
@@ -90,7 +101,7 @@
 
     def own_weights(q, depth):
         return pltpu.make_async_copy(
-            proj_hbm.at[:depth, q * thin:(q + 1) * thin], wall.at[q, :depth, :], in_sem.at[3 + q]
+            proj_hbm.at[:depth, q * thin:(q + 1) * thin], wall.at[q, :depth, :], in_sem.at[5 + q]
         )
 
     def each_own_weights(act):
@@ -106,15 +117,21 @@
                     act(own_weights(q, near * width))
 
     each_own_weights(lambda copy: copy.start())
-    for copy in kv_copies:
-        copy.wait()
+    with jax.named_scope("kvload"):
+        for copy in kv_copies:
+            copy.wait()
     with jax.named_scope("barrier"):
         pl.semaphore_wait(barrier, greeted)
 
     def hop(buf, send, recv, side, zs, cs, g, cut=None):
         target = ({"seq": jnp.minimum(z + 1, S - 1)}, {"seq": jnp.maximum(z - 1, 0)}, {"sub": (c + 1) % C})[side]
         index = zs * C + cs
-        block = buf.at[index, g] if cut is None else buf.at[index, g, :, cut]
+        if buf is kvbuf:
+            block = buf.at[index, g]
+        else:
+            if cut is None:
+                cut = pl.ds(pl.multiple_of(g % R * cut_width, HEAD_WIDTH), cut_width)
+            block = buf.at[index, g // R, :, cut]
         return pltpu.make_async_remote_copy(
             src_ref=block,
             dst_ref=block,
@@ -124,16 +141,18 @@
             device_id_type=MESH,
         )
 
-    def launch(buf, send, recv, g, lo, hi, cut=None):
-        @pl.when(z + 1 <= hi)
+    def launch(buf, send, recv, g, lo, hi, cut=None, ways=None):
+        inward_too, edgeward_too = ways or (True, True)
+
+        @pl.when((z + 1 <= hi) & jnp.where(inward > 0, inward_too, edgeward_too))
         def _():
             hop(buf, send, recv, 0, z, c, g, cut).start()
 
-        @pl.when(z - 1 >= lo)
+        @pl.when((z - 1 >= lo) & jnp.where(inward < 0, inward_too, edgeward_too))
         def _():
             hop(buf, send, recv, 1, z, c, g, cut).start()
 
-        if C > 1:
+        if C > 1 and inward_too:
             @pl.when((z >= lo) & (z <= hi))
             def _():
                 hop(buf, send, recv, 2, z, c, g, cut).start()
@@ -216,14 +235,24 @@
         def _():
             launch(kvbuf, kv_send, kv_recv, jnp.minimum(s + 2, G - 1), 0, S - 1)
 
+        def either(d, ahead):
+            g = s + 1 - d + ahead
+
+            @pl.when((g >= 0) & (g < G))
+            def _():
+                at = jnp.clip(g, 0, G - 1)
+
+                @pl.when((inward > 0) == (ahead > 0))
+                def _():
+                    relay_right(kvbuf, kv_send, kv_recv, d, at, 0, S - 1)
+
+                @pl.when((inward < 0) == (ahead > 0))
+                def _():
+                    relay_left(kvbuf, kv_send, kv_recv, d, at, 0, S - 1)
+
         def one(d):
-            g = s + 1 - d
-
-            @pl.when((g >= 0) & (g < G))
-            def _():
-                at = jnp.clip(g, 0, G - 1)
-                relay_right(kvbuf, kv_send, kv_recv, d, at, 0, S - 1)
-                relay_left(kvbuf, kv_send, kv_recv, d, at, 0, S - 1)
+            either(d, 1)
+            either(d, 0)
 
         with jax.named_scope("wave"):
             loop(1, S, one)
@@ -239,6 +268,8 @@
             loop(min(2, G), G, lambda g: launch(kvbuf, kv_send, kv_recv, g, 0, S - 1))
             loop(0, pieces, lambda i: w_out(i).start())
 
+    for copy in table_copies:
+        copy.wait()
     half_rows = total // order_ref.shape[0]
     per_device = rows // half_rows
     lane = lax.broadcasted_iota(jnp.int32, (1, total), 1)
@@ -279,10 +310,10 @@
             o = jnp.dot(w.astype(jnp.bfloat16), value, preferred_element_type=jnp.float32)
             o = (o / amount).astype(jnp.bfloat16)
             o = jnp.concatenate([o[k * rows:(k + 1) * rows] for k in range(pack)], axis=1)
-            att_out[:, pl.ds(at, span)] = o
             cut = pl.ds(pl.multiple_of(b * span, span), span)
             attbuf[own, g, :, cut] = o
-            launch(attbuf, at_send, at_recv, g, *reach(g), cut)
+            e = g * R + b * R // steps
+            launch(attbuf, at_send, at_recv, e, *reach(e), cut, (True, False))
 
             turn = g * steps + b - lead
 
@@ -302,14 +333,21 @@
             device_id_type=MESH,
         )
 
-    def multiply(zb, u, weights, g0, g1):
-        summed = jnp.zeros((C * rows, thin), jnp.float32)
+    def dots(summed, zb, u, weights, g0, g1, base):
         for g in range(g0, g1):
             summed = summed + jnp.dot(
                 attbuf[pl.ds(zb * C, C), g].reshape(C * rows, width),
-                weights[u % Q, (g - g0) * width:(g - g0 + 1) * width, :],
+                weights[u % Q, (g - base) * width:(g - base + 1) * width, :],
                 preferred_element_type=jnp.float32,
             )
+        return summed
+
+    def multiply_part(zb, u, weights, g0, g1, base):
+        acc[u] = dots(jnp.zeros((C * rows, thin), jnp.float32), zb, u, weights, g0, g1, base)
+
+    def multiply(zb, u, weights, g0, g1, base, more=False):
+        start = acc[u] if more else jnp.zeros((C * rows, thin), jnp.float32)
+        summed = dots(start, zb, u, weights, g0, g1, base)
         summed = summed.astype(jnp.bfloat16)
         for k in range(C):
             t = zb * C + k
@@ -386,27 +424,41 @@
                 def _():
                     result_copy(t, u).start()
 
+    def arrive(zb, e0, e1):
+        with jax.named_scope("arrive"):
+            loop(e0, e1, lambda e: from_partner(attbuf, at_send, at_recv, zb, e))
+
     def multiply_all(zb):
         @pl.when(inner)
         def _():
-            with jax.named_scope("arrive"):
-                loop(0, G, lambda g: from_partner(attbuf, at_send, at_recv, zb, g))
+            arrive(zb, 0, E)
             with jax.named_scope("mult"):
-                loop(0, Q, lambda u: multiply(zb, u, wall, 0, G))
+                loop(0, Q, lambda u: multiply(zb, u, wall, 0, G, 0))
 
         if hub and near:
             @pl.when(outer)
             def _():
-                with jax.named_scope("arrive"):
-                    loop(0, near, lambda g: from_partner(attbuf, at_send, at_recv, zb, g))
+                arrive(zb, 0, near * R)
                 with jax.named_scope("multend"):
-                    loop(0, Q, lambda u: multiply(zb, u, wall, 0, near))
+                    loop(0, Q, lambda u: multiply(zb, u, wall, 0, near, 0))
 
     def multiply_extra(zb):
         @pl.when(is_hub)
         def _():
             with jax.named_scope("extra"):
-                loop(Q, 2 * Q, lambda u: multiply(zb, u, wext, near, G))
+                loop(Q, 2 * Q, lambda u: multiply(zb, u, wext, near, G, near))
+
+    def multiply_most(zb):
+        arrive(zb, 0, (G - 1) * R)
+        with jax.named_scope("most"):
+            loop(0, Q, lambda u: multiply_part(zb, u, wall, 0, G - 1, 0))
+            loop(Q, 2 * Q, lambda u: multiply_part(zb, u, wext, near, G - 1, near))
+
+    def multiply_last(zb):
+        arrive(zb, (G - 1) * R, E)
+        with jax.named_scope("last"):
+            loop(0, Q, lambda u: multiply(zb, u, wall, G - 1, G, 0, True))
+            loop(Q, 2 * Q, lambda u: multiply(zb, u, wext, G - 1, G, near, True))
 
     def reduce_extra(zb):
         @pl.when(is_hub)
@@ -423,9 +475,9 @@
     def by_slot(k, act, self_slot):
         def pick(which):
             since = jnp.where(which == 2, k - side_lag, k)
-            d = jnp.where(which == 0, 0, since // G + 1)
+            d = jnp.where(which == 0, 0, since // E + 1)
             zb = z + jnp.where(which == 2, -inward, inward) * d
-            due = jnp.where(which == 0, k == self_slot, (since >= 0) & (since % G == G - 1))
+            due = jnp.where(which == 0, k == self_slot, (since >= 0) & (since % E == E - 1))
 
             @pl.when(due & (zb >= 0) & (zb < S))
             def _():
@@ -434,60 +486,187 @@
         loop(0, 3, pick)
 
     def relay_slot(k, rightward):
-        d, g = k // G + 1, k % G
+        d, g = k // E + 1, k % E
         move = relay_right if rightward else relay_left
         move(attbuf, at_send, at_recv, d, g, *reach(g))
 
+    @pl.when(inward > 0)
+    def _():
+        relay_right(kvbuf, kv_send, kv_recv, 1, 0, 0, S - 1)
+
+    @pl.when(inward < 0)
+    def _():
+        relay_left(kvbuf, kv_send, kv_recv, 1, 0, 0, S - 1)
+
     loop(0, S - 1, wave)
     q_copy.wait()
+
+    def att_copy(g):
+        return pltpu.make_async_copy(
+            attbuf.at[own, g], att_hbm.at[:, pl.ds(pl.multiple_of(g * width, width), width)], out_sem.at[2 + g]
+        )
 
     def head_step(g):
         with jax.named_scope("attention"):
             attention(g)
+        att_copy(g).start()
+        loop(g * R, (g + 1) * R, lambda e: launch(attbuf, at_send, at_recv, e, *reach(e), None, (False, True)))
+
         if hub:
             for k in range(2):
-                @pl.when(is_hub & (g > 0) & ((g - 1) * 2 + k < pieces))
+                @pl.when(is_hub & (g < G - 1) & (g * 2 + 1 + k < pieces))
                 def _():
-                    w_relay((g - 1) * 2 + k)
+                    w_relay(g * 2 + 1 + k)
+
+    if hub:
+        @pl.when(is_hub)
+        def _():
+            w_relay(0)
 
     loop(0, G, head_step)
     each_own_weights(lambda copy: copy.wait())
+
+    far = jnp.where(z < S // 2, S - 1 - z, z)
 
     def slot_step(k):
         if hub:
             @pl.when(is_hub & (k == min(1, side_lag)))
             def _():
-                loop(min(pieces, 2 * (G - 1)), pieces, w_relay)
+                loop(min(pieces, 2 * G - 1), pieces, w_relay)
 
         with jax.named_scope("arelay"):
             for rightward in (False, True):
-                inner_side = (inward < 0) if rightward else (inward > 0)
-                at = jnp.where(inner_side, k, k - side_lag)
-
-                @pl.when(at >= 0)
+                @pl.when((k >= side_lag) & ((inward > 0) if rightward else (inward < 0)))
                 def _():
-                    relay_slot(jnp.maximum(at, 0), rightward)
+                    relay_slot(jnp.maximum(k - side_lag, 0), rightward)
+
+            for rightward in (False, True):
+                @pl.when((inward < 0) if rightward else (inward > 0))
+                def _():
+                    relay_slot(k, rightward)
 
         if hub:
-            @pl.when(is_hub & (k == side_lag))
+            @pl.when(is_hub & (k == extra_slot))
             def _():
                 with jax.named_scope("wother"):
                     for t in range(1, Y):
                         loop(0, pieces, lambda i: w_pass(i, 1, (y + t) % Y).wait_recv())
 
-        by_slot(k, multiply_all, 0)
+        split = hub and G > 1
+        last_slot = far * E - 1
+
+        def unsplit(act):
+            def guarded(zb):
+                if split:
+                    @pl.when(jnp.logical_not(is_hub & (k == last_slot) & (zb == z + inward * far)))
+                    def _():
+                        act(zb)
+                else:
+                    act(zb)
+
+            return guarded
+
+        by_slot(k, unsplit(multiply_all), 0)
         if hub:
-            by_slot(k, multiply_extra, side_lag)
-
-        @pl.when(k > 0)
-        def _():
-            by_slot(k - 1, reduce_all, 0)
-
-    slots = (S - 1) * G + side_lag
+            by_slot(k, unsplit(multiply_extra), extra_slot)
+        if split:
+            @pl.when(is_hub & (k == last_slot - R))
+            def _():
+                multiply_most(z + inward * far)
+
+            @pl.when(is_hub & (k == last_slot))
+            def _():
+                multiply_last(z + inward * far)
+
+        def reduce_soon(zb):
+            @pl.when(jnp.logical_not(is_hub & (zb == z + inward)))
+            def _():
+                reduce_all(zb)
+
+        @pl.when(k > 1)
+        def _():
+            by_slot(k - 2, reduce_soon if hub else reduce_all, self_done)
+
+        if hub:
+            @pl.when(is_hub & (k == E + side_lag))
+            def _():
+                reduce_all(z + inward)
+
+    slots = jnp.maximum(far * E, (S - 1 - far) * E + side_lag)
     loop(0, slots, slot_step)
-    by_slot(slots - 1, reduce_all, 0)
     if hub:
-        loop(0, slots, lambda k: by_slot(k, reduce_extra, side_lag))
+        reduce_extra(z)
+        reduce_extra(z + inward)
+        reduce_extra(z - inward)
+    loop(slots - 2, slots, lambda k: by_slot(k, reduce_all, self_done))
+    if hub:
+        def reduce_far(d):
+            for way in (-inward, inward):
+                zb = z + way * d
+
+                @pl.when((zb >= 0) & (zb < S))
+                def _():
+                    reduce_extra(jnp.clip(zb, 0, S - 1))
+
+        loop(2, S - 1, reduce_far)
+
+    def finish(i):
+        zs, g = i // G, i % G
+        drain(kvbuf, kv_send, kv_recv, zs, g, 0, S - 1)
+
+    def finish_att(i):
+        zs, e = i // E, i % E
+        drain(attbuf, at_send, at_recv, zs, e, *reach(e))
+
+    with jax.named_scope("drain"):
+        loop(0, S * G, finish)
+        loop(0, S * E, finish_att)
+
+    def each_result(u, act):
+        def one(s):
+            act(s * H + h, u)
+
+        loop(0, n // H, one)
+
+    def finish_x(u):
+        def finish_one(t):
+            @pl.when(t % H != h)
+            def _():
+                x_copy(t, u).wait_send()
+
+        @pl.when(((u < Q) & ((inner | outer) if near else inner)) | ((u >= Q) & is_hub))
+        def _():
+            loop(0, n, finish_one)
+            if hub and near:
+                @pl.when(outer)
+                def _():
+                    each_result(u, lambda t, u: merge_copy(t, u).wait_send())
+
+    def finish_results(u):
+        home, slot, q = place_of(u)
+
+        def finish_one(t, u):
+            @pl.when(jnp.logical_not((t == own) & (home == h)))
+            def _():
+                result_copy(t, u).wait_send()
+
+        @pl.when(inner & ((u < Q) | is_hub))
+        def _():
+            each_result(u, finish_one)
+
+    units = Q * (2 if hub else 1)
+    loop(0, units, finish_x)
+
+    if hub:
+        @pl.when(outer)
+        def _():
+            loop(0, pieces, lambda i: w_out(i).wait_send())
+
+        @pl.when(is_hub)
+        def _():
+            for k in range(1, Y):
+                loop(0, pieces, lambda i: w_pass(i, k, y).wait_send())
+    loop(0, G, lambda g: att_copy(g).wait())
 
     res_copy.wait()
     squares = jnp.zeros((rows, 1), jnp.float32)
@@ -513,6 +692,7 @@
             squares = squares + jnp.sum(wide * wide, axis=-1, keepdims=True)
 
     ebuf[h] = jnp.broadcast_to(squares, (rows, 128))
+    hidden_copy = pltpu.make_async_copy(hidden_out, hidden_hbm, out_sem.at[0])
 
     def share(k, side):
         other = (h + k) % H if side == 0 else (h + H - k) % H
@@ -524,6 +704,9 @@
 
     for k in range(1, H):
         share(k, 0).start()
+    hidden_copy.start()
+    gain_copy.wait()
+    loop(0, units, finish_results)
     with jax.named_scope("energy"):
         for k in range(1, H):
             share(k, 1).wait_recv()
@@ -531,56 +714,32 @@
     for k in range(1, H):
         energy = energy + ebuf[k]
     inverse = lax.rsqrt(energy[:, 0:1] / (H * res_ref.shape[1]) + 1e-06)
-    gain_copy.wait()
     for b in range(blocks):
         where = slice(b * Q * thin, (b + 1) * Q * thin)
         normed_out[:, where] = (
             hidden_out[:, where].astype(jnp.float32) * inverse * gain_ref[:, where]
         ).astype(jnp.bfloat16)
-
+    normed_copy = pltpu.make_async_copy(normed_out, normed_hbm, out_sem.at[1])
+    normed_copy.start()
     for k in range(1, H):
         share(k, 0).wait_send()
-
-    def finish(i):
-        zs, g = i // G, i % G
-        drain(kvbuf, kv_send, kv_recv, zs, g, 0, S - 1)
-        drain(attbuf, at_send, at_recv, zs, g, *reach(g))
-
-    with jax.named_scope("drain"):
-        loop(0, S * G, finish)
-
-    def finish_results(u):
-        home, slot, q = place_of(u)
-
-        def finish_one(t):
-            @pl.when(t % H != h)
-            def _():
-                x_copy(t, u).wait_send()
-
-            @pl.when(inner & (t % H == h) & jnp.logical_not((t == own) & (home == h)))
-            def _():
-                result_copy(t, u).wait_send()
-
-            if hub and near:
-                @pl.when(outer & (t % H == h))
-                def _():
-                    merge_copy(t, u).wait_send()
-
-        @pl.when(((u < Q) & ((inner | outer) if near else inner)) | ((u >= Q) & is_hub))
-        def _():
-            loop(0, n, finish_one)
-
-    loop(0, Q * (2 if hub else 1), finish_results)
-
-    if hub:
-        @pl.when(outer)
-        def _():
-            loop(0, pieces, lambda i: w_out(i).wait_send())
-
-        @pl.when(is_hub)
-        def _():
-            for k in range(1, Y):
-                loop(0, pieces, lambda i: w_pass(i, k, y).wait_send())
+    hidden_copy.wait()
+    normed_copy.wait()
+
+
+def deliver(*refs):
+    count = len(refs) // 3
+    given, out, held = refs[:count], refs[count:2 * count], refs[2 * count:3 * count]
+    sem = refs[3 * count]
+    fetch = [pltpu.make_async_copy(given[i], held[i], sem.at[0, i]) for i in range(count)]
+    store = [pltpu.make_async_copy(held[i], out[i], sem.at[1, i]) for i in range(count)]
+    for copy in fetch:
+        copy.start()
+    for i in range(count):
+        fetch[i].wait()
+        store[i].start()
+    for copy in store:
+        copy.wait()
 
 
 def shards(dims, queries, keys, values, half_order, frame_lengths, out_proj, residual_in, norm_gain):
@@ -596,21 +755,26 @@
     near = G // 2
     thin = cols // Q
     U = Q * (2 if hub else 1)
+    E = G * (2 if width // HEAD_WIDTH % 4 == 0 else 1)
     hbm = pl.BlockSpec(memory_space=pltpu.HBM)
     vmem = pl.BlockSpec(memory_space=pltpu.VMEM)
-    smem = pl.BlockSpec(memory_space=pltpu.SMEM)
     dma = pltpu.SemaphoreType.DMA
     bf16, f32 = jnp.bfloat16, jnp.float32
-    return pl.pallas_call(
+    made = pl.pallas_call(
         functools.partial(kernel, (S, C, H, G, Y, Q, NJ, hub, near)),
         out_shape=(
             jax.ShapeDtypeStruct(queries.shape, bf16),
             jax.ShapeDtypeStruct(residual_in.shape, bf16),
             jax.ShapeDtypeStruct(residual_in.shape, bf16),
         ),
-        in_specs=[smem, smem, hbm, hbm, hbm, hbm, hbm, hbm],
-        out_specs=(vmem, vmem, vmem),
+        in_specs=[hbm, hbm, hbm, hbm, hbm, hbm, hbm, hbm],
+        out_specs=(hbm, hbm, hbm),
         scratch_shapes=[
+            pltpu.SMEM(half_order.shape, jnp.int32),
+            pltpu.SMEM(frame_lengths.shape, jnp.int32),
+            pltpu.VMEM(residual_in.shape, bf16),
+            pltpu.VMEM(residual_in.shape, bf16),
+            pltpu.VMEM((U, C * rows, thin), f32),
             pltpu.VMEM((n, G, 2, rows, HEAD_WIDTH), bf16),
             pltpu.VMEM((n, G, rows, width), bf16),
             pltpu.VMEM((Q, deep, thin), bf16),
@@ -625,12 +789,13 @@
             pltpu.VMEM((Q, n // H, rows, thin), bf16),
             pltpu.VMEM((n // H, Q, rows, thin), bf16),
             pltpu.VMEM((H, rows, 128), f32),
-            dma((3 + Q,)),
+            dma((5 + Q,)),
+            dma((2 + G,)),
             dma((G, 2)),
             dma((3, S, G)),
             dma((n, G)),
-            dma((3, S, G)),
-            dma((n, G)),
+            dma((3, S, E)),
+            dma((n, E)),
             dma((U, n)),
             dma((U, n // H, H)),
             dma((U, n // H)),
@@ -643,9 +808,16 @@
             dma((H,)),
         ],
         compiler_params=pltpu.CompilerParams(
-            collective_id=0, has_side_effects=True, vmem_limit_bytes=51 * 1024 * 1024
+            collective_id=0, has_side_effects=True, vmem_limit_bytes=60 * 1024 * 1024
         ),
     )(half_order, frame_lengths, queries, keys, values, out_proj, residual_in, norm_gain[None, :])
+    return pl.pallas_call(
+        deliver,
+        out_shape=tuple(jax.ShapeDtypeStruct(a.shape, bf16) for a in made),
+        in_specs=[hbm] * 3,
+        out_specs=(hbm,) * 3,
+        scratch_shapes=[pltpu.VMEM(a.shape, bf16) for a in made] + [dma((2, 3))],
+    )(*made)
 
 
 def solution(mesh):

time: 103 us -> 94.7 us (0.919)
  local copies, waits for them, and re-layouts: 7.41 us -> 0 us
  Pallas kernels: 95.1 us -> 93.9 us
    unnamed x15 -> x0, local copies, waits for them, and re-layouts: 7.41 us -> none
    pallas_call x1, Pallas kernels: 95.1 us -> 91.3 us  [shards(): pl.pallas_call(functools.partial(kernel, (S, C, H, G, Y, Q, NJ, hub, near...]
    pallas_call x0 -> x1, Pallas kernels: none -> 2.59 us  [shards(): pl.pallas_call(deliver, out_shape=tuple((jax.ShapeDtypeStruct(a.shape, bf...]
where the time goes in v2:
time: 94.7 us; the launch traced here: 94.5 us
  Pallas kernels  93.9 us (99%)
    pallas_call x1, Pallas kernels, shards(): pl.pallas_call(functools.partial(kernel, (S, C, H, G, Y, Q, NJ, hub, near...  91.3 us
    pallas_call x1, Pallas kernels, shards(): pl.pallas_call(deliver, out_shape=tuple((jax.ShapeDtypeStruct(a.shape, bf...  2.59 us

profile of v2, /device:TPU:0, one launch (start us, length us, event | category | flops | bytes accessed | tf_op | source)
XLA Modules:
  0.0 94.5 jit_solution(5474102049173696335)
XLA Ops:
  0.6 91.3 %shard_map.103 = (bf16[128,4096]{1,0:T(8,128)(2,1)}, bf16[128,2048]{1,0:T(8,128)(2,1)}, bf16[128,2048]{1,0:T(8,128)(2,1)}) custom-call(s32[16]{0:T(128)} %order_hbm.1, s32[8]{0:T(128)} %frames_hbm.1, bf16[128,4096]{1,0:T(8,128)(2,1)} %q_hbm.1, bf16[128,512]{1,0:T(8,128)(2,1)} %k_hbm.1, bf16[128,512]{1,0:T(8,128)(2,1)} %v_hbm.1, bf16[4096,512]{1,0:T(8,128)(2,1)} %proj_hbm.1, ...), custom_call_target="tpu_custom_call" | custom-call | tf_op jit(solution)/shard_map/pallas_call | solution.py:763
  91.9 2.6 %shard_map.104 = (bf16[128,4096]{1,0:T(8,128)(2,1)}, bf16[128,2048]{1,0:T(8,128)(2,1)}, bf16[128,2048]{1,0:T(8,128)(2,1)}) custom-call(bf16[128,4096]{1,0:T(8,128)(2,1)} %get-tuple-element.6.refs_0_, bf16[128,2048]{1,0:T(8,128)(2,1)} %get-tuple-element.7.refs_1_, bf16[128,2048]{1,0:T(8,128)(2,1)} %get-tuple-element.8.refs_2_), custom_call_target="tpu_custom_call" | custom-call | tf_op jit(solution)/shard_map/pallas_call | solution.py:814

commit v3 on v2

--- a/solution.py
+++ b/solution.py
@@ -22,9 +22,9 @@
 
 def kernel(dims, order_hbm, frames_hbm, q_hbm, k_hbm, v_hbm, proj_hbm, res_hbm, gain_hbm,
            att_hbm, hidden_hbm, normed_hbm,
-           order_ref, frames_ref, hidden_out, normed_out, acc, kvbuf, attbuf, wall, wext, q_ref, res_ref, gain_ref, bias, pbuf, xbuf, obuf, mbuf, retbuf, ebuf,
-           in_sem, out_sem, kv_in, kv_send, kv_recv, at_send, at_recv, x_send, x_recv, ret_send, ret_recv, m_recv,
-           w_send, w_recv, wf_send, en_send, en_recv):
+           order_ref, frames_ref, hidden_out, normed_out, kvbuf, attbuf, wall, wext, q_ref, res_ref, gain_ref, bias, pbuf, xbuf, obuf, mbuf, retbuf, ebuf,
+           in_sem, out_sem, kv_in, kv_send, kv_recv, at_send, at_recv, at_part, x_send, x_recv, ret_send, ret_recv,
+           m_recv, w_send, w_recv, wy_recv, wf_send, en_send, en_recv):
     S, C, H, G, Y, Q, NJ, hub, near = dims
     n = S * C
     blocks = n // H
@@ -43,9 +43,10 @@
     R = 2 if steps % 2 == 0 else 1
     E = G * R
     cut_width = width // R
-    side_lag = E // 2
+    side_lag = min(2, E - 1)
+    mid = min(2, pieces - NJ)
     self_done = E // 2
-    extra_slot = min(side_lag + 2, E - 1)
+    extra_slot = min(side_lag + 4, E - 1)
     y, z = lax.axis_index("groups"), lax.axis_index("seq")
     c, h = lax.axis_index("sub"), lax.axis_index("heads")
     own = z * C + c
@@ -56,10 +57,22 @@
     hub_of_edge = jnp.where(z < S // 2, 1, S - 2)
     inward = jnp.where(z < S // 2, 1, -1)
 
-    def reach(g):
+    def is_edge(zs):
+        return (zs == 0) | (zs == S - 1)
+
+    def rows_piece(e):
+        rest = jnp.maximum(e - near * R, 0)
+        first = e < near * R
+        return jnp.where(first, e % R, rest // (G - near)), jnp.where(first, e // R, near + rest % (G - near))
+
+    def part_of(e):
+        return jnp.maximum(e - near * R, 0) // (G - near)
+
+    def reach(e):
         if not hub:
             return 0, S - 1
-        return jnp.where(g < near * R, 0, 1), jnp.where(g < near * R, S - 1, S - 2)
+        wide = e < near * R
+        return jnp.where(wide, 0, 1), jnp.where(wide, S - 1, S - 2)
 
     kv_copies = []
     for g in range(G):
@@ -123,11 +136,21 @@
     with jax.named_scope("barrier"):
         pl.semaphore_wait(barrier, greeted)
 
-    def hop(buf, send, recv, side, zs, cs, g, cut=None):
+    def hop(buf, send, recv, side, zs, cs, g, cut=None, by_rows=False):
         target = ({"seq": jnp.minimum(z + 1, S - 1)}, {"seq": jnp.maximum(z - 1, 0)}, {"sub": (c + 1) % C})[side]
         index = zs * C + cs
+        if side < 2:
+            landing = recv.at[zs, g]
+        elif buf is kvbuf:
+            landing = recv.at[S, g]
+        else:
+            landing = at_part.at[zs, part_of(g)]
         if buf is kvbuf:
             block = buf.at[index, g]
+        elif by_rows:
+            size = rows // R
+            band, group = rows_piece(g)
+            block = buf.at[index, group, pl.ds(pl.multiple_of(band * size, size), size), :]
         else:
             if cut is None:
                 cut = pl.ds(pl.multiple_of(g % R * cut_width, HEAD_WIDTH), cut_width)
@@ -135,27 +158,39 @@
         return pltpu.make_async_remote_copy(
             src_ref=block,
             dst_ref=block,
-            send_sem=send.at[side, zs, g],
-            recv_sem=recv.at[index, g],
+            send_sem=send.at[side, zs],
+            recv_sem=landing,
             device_id=target,
             device_id_type=MESH,
         )
 
-    def launch(buf, send, recv, g, lo, hi, cut=None, ways=None):
-        inward_too, edgeward_too = ways or (True, True)
+    def begin(buf, send, recv, side, zs, cs, g):
+        if buf is kvbuf or not hub:
+            hop(buf, send, recv, side, zs, cs, g).start()
+        else:
+            @pl.when(is_edge(zs))
+            def _():
+                hop(buf, send, recv, side, zs, cs, g, by_rows=True).start()
+
+            @pl.when(jnp.logical_not(is_edge(zs)))
+            def _():
+                hop(buf, send, recv, side, zs, cs, g).start()
+
+    def launch(buf, send, recv, g, lo, hi, cut=None, ways=(True, True), by_rows=False):
+        inward_too, edgeward_too = ways
 
         @pl.when((z + 1 <= hi) & jnp.where(inward > 0, inward_too, edgeward_too))
         def _():
-            hop(buf, send, recv, 0, z, c, g, cut).start()
+            hop(buf, send, recv, 0, z, c, g, cut, by_rows).start()
 
         @pl.when((z - 1 >= lo) & jnp.where(inward < 0, inward_too, edgeward_too))
         def _():
-            hop(buf, send, recv, 1, z, c, g, cut).start()
+            hop(buf, send, recv, 1, z, c, g, cut, by_rows).start()
 
         if C > 1 and inward_too:
             @pl.when((z >= lo) & (z <= hi))
             def _():
-                hop(buf, send, recv, 2, z, c, g, cut).start()
+                hop(buf, send, recv, 2, z, c, g, cut, by_rows).start()
 
     def relay_right(buf, send, recv, d, g, lo, hi):
         @pl.when((z - d >= 0) & (z >= lo) & (z <= hi))
@@ -164,10 +199,10 @@
 
             @pl.when(z + 1 <= hi)
             def _():
-                hop(buf, send, recv, 0, z - d, c, g).start()
+                begin(buf, send, recv, 0, z - d, c, g)
 
             if C > 1:
-                hop(buf, send, recv, 2, z - d, c, g).start()
+                begin(buf, send, recv, 2, z - d, c, g)
 
     def relay_left(buf, send, recv, d, g, lo, hi):
         @pl.when((z + d < S) & (z >= lo) & (z <= hi))
@@ -176,28 +211,48 @@
 
             @pl.when(z - 1 >= lo)
             def _():
-                hop(buf, send, recv, 1, z + d, c, g).start()
+                begin(buf, send, recv, 1, z + d, c, g)
 
             if C > 1:
-                hop(buf, send, recv, 2, z + d, c, g).start()
-
-    def from_partner(buf, send, recv, zs, g):
-        if C > 1:
-            hop(buf, send, recv, 2, zs, (c + 1) % C, g).wait_recv()
-
-    def drain(buf, send, recv, zs, g, lo, hi):
-        @pl.when((zs <= z) & (z + 1 <= hi))
-        def _():
-            hop(buf, send, recv, 0, zs, c, g).wait_send()
-
-        @pl.when((zs >= z) & (z - 1 >= lo))
-        def _():
-            hop(buf, send, recv, 1, zs, c, g).wait_send()
-
-        if C > 1:
-            @pl.when((z >= lo) & (z <= hi))
-            def _():
-                hop(buf, send, recv, 2, zs, c, g).wait_send()
+                begin(buf, send, recv, 2, z + d, c, g)
+
+    def sized(ref, send_sem, recv_sem):
+        return pltpu.make_async_remote_copy(
+            src_ref=ref, dst_ref=ref, send_sem=send_sem, recv_sem=recv_sem,
+            device_id={"sub": (c + 1) % C}, device_id_type=MESH,
+        )
+
+    def landed(zs, part, count):
+        if C > 1 and count:
+            some = attbuf.at[pl.ds(0, count), 0, pl.ds(0, rows // R), :]
+            sized(some, at_send.at[0, zs], at_part.at[zs, part]).wait_recv()
+
+    def drain(buf, send, zs, kept):
+        index = zs * C + c
+
+        def done(side, cond, full):
+            block = buf.at[index] if full else buf.at[index, pl.ds(0, kept)]
+
+            @pl.when(cond)
+            def _():
+                sized(block, send.at[side, zs], send.at[side, zs]).wait_send()
+
+        right, left = (zs <= z) & (z + 1 < S), (zs >= z) & (z > 0)
+        if kept is None:
+            done(0, right, True)
+            done(1, left, True)
+            if C > 1:
+                done(2, z >= 0, True)
+        else:
+            done(0, right & (z + 1 < S - 1), True)
+            done(1, left & (z > 1), True)
+            if C > 1:
+                done(2, inner, True)
+            if kept:
+                done(0, right & (z + 1 == S - 1), False)
+                done(1, left & (z == 1), False)
+                if C > 1:
+                    done(2, outer, False)
 
     def w_block(i, side):
         q, j = i // NJ, i % NJ
@@ -211,24 +266,29 @@
                 pl.ds(pl.multiple_of(q * thin, thin), thin),
             ],
             dst_ref=wext.at[q, pl.ds(pl.multiple_of(at, piece_rows), piece_rows), :],
-            send_sem=w_send.at[i], recv_sem=w_recv.at[y, i],
+            send_sem=w_send.at[0], recv_sem=w_recv.at[i],
             device_id={"seq": hub_of_edge}, device_id_type=MESH,
         )
 
-    def w_pass(i, k, side):
-        q, at = w_block(i, side)
+    def w_pass(i, k):
+        q, at = w_block(i, y)
         block = wext.at[q, pl.ds(pl.multiple_of(at, piece_rows), piece_rows), :]
         return pltpu.make_async_remote_copy(
             src_ref=block, dst_ref=block,
-            send_sem=wf_send.at[k - 1, i], recv_sem=w_recv.at[side, i],
+            send_sem=wf_send.at[k - 1], recv_sem=wy_recv.at[Y - 1 - k, q],
             device_id={"groups": (y + k) % Y}, device_id_type=MESH,
         )
 
     def w_relay(i):
         with jax.named_scope("wwait"):
-            w_pass(i, 1, y).wait_recv()
+            w_out(i).wait_recv()
         for k in range(1, Y):
-            w_pass(i, k, y).start()
+            w_pass(i, k).start()
+
+    def w_landed(q):
+        for k in range(1, Y):
+            some = wext.at[q, pl.ds(0, part_rows), :]
+            sized(some, wf_send.at[k - 1], wy_recv.at[k - 1, q]).wait_recv()
 
     def wave(s):
         @pl.when((s + 2 < G) & (inner if hub else True))
@@ -259,14 +319,15 @@
 
     def kv_partner(g):
         with jax.named_scope("kvpartner"):
-            loop(0, S, lambda s: from_partner(kvbuf, kv_send, kv_recv, s, g))
+            if C > 1:
+                sized(kvbuf.at[pl.ds(0, S), g], kv_send.at[0, 0], kv_recv.at[S, g]).wait_recv()
 
     loop(0, min(2, G), lambda g: launch(kvbuf, kv_send, kv_recv, g, 0, S - 1))
     if hub:
         @pl.when(outer)
         def _():
             loop(min(2, G), G, lambda g: launch(kvbuf, kv_send, kv_recv, g, 0, S - 1))
-            loop(0, pieces, lambda i: w_out(i).start())
+            loop(0, NJ, lambda i: w_out(i).start())
 
     for copy in table_copies:
         copy.wait()
@@ -313,7 +374,10 @@
             cut = pl.ds(pl.multiple_of(b * span, span), span)
             attbuf[own, g, :, cut] = o
             e = g * R + b * R // steps
-            launch(attbuf, at_send, at_recv, e, *reach(e), cut, (True, False))
+
+            @pl.when(inner)
+            def _():
+                launch(attbuf, at_send, at_recv, e, *reach(e), cut, (True, False))
 
             turn = g * steps + b - lead
 
@@ -323,31 +387,38 @@
 
         loop(0, steps, few_heads)
 
-    def x_copy(t, u):
+    def span_of(part):
+        if part is None:
+            return slice(0, rows)
+        size = rows // R
+        return slice(part * size, (part + 1) * size)
+
+    extra_slots = max(1, C // H)
+
+    def x_slot(t, part):
+        return t // H if not part else n // H + (part - 1) * extra_slots + t // H % extra_slots
+
+    def x_copy(t, u, part=None):
+        where = span_of(part)
         return pltpu.make_async_remote_copy(
-            src_ref=pbuf.at[u, t],
-            dst_ref=xbuf.at[u, t // H, h],
-            send_sem=x_send.at[u, t],
-            recv_sem=x_recv.at[u, t // H, h],
+            src_ref=pbuf.at[u, t, where],
+            dst_ref=xbuf.at[u, t // H, h, where],
+            send_sem=x_send.at[u],
+            recv_sem=x_recv.at[u, x_slot(t, part), jnp.minimum((h - t % H - 1) % H, max(H - 2, 0))],
             device_id={"heads": t % H},
             device_id_type=MESH,
         )
 
-    def dots(summed, zb, u, weights, g0, g1, base):
+    def multiply(zb, u, weights, g0, g1, base, part=None):
+        where = span_of(part)
+        tall = where.stop - where.start
+        summed = jnp.zeros((C * tall, thin), jnp.float32)
         for g in range(g0, g1):
             summed = summed + jnp.dot(
-                attbuf[pl.ds(zb * C, C), g].reshape(C * rows, width),
+                attbuf[pl.ds(zb * C, C), g, where].reshape(C * tall, width),
                 weights[u % Q, (g - base) * width:(g - base + 1) * width, :],
                 preferred_element_type=jnp.float32,
             )
-        return summed
-
-    def multiply_part(zb, u, weights, g0, g1, base):
-        acc[u] = dots(jnp.zeros((C * rows, thin), jnp.float32), zb, u, weights, g0, g1, base)
-
-    def multiply(zb, u, weights, g0, g1, base, more=False):
-        start = acc[u] if more else jnp.zeros((C * rows, thin), jnp.float32)
-        summed = dots(start, zb, u, weights, g0, g1, base)
         summed = summed.astype(jnp.bfloat16)
         for k in range(C):
             t = zb * C + k
@@ -355,23 +426,24 @@
 
             @pl.when(mine)
             def _():
-                xbuf[u, t // H, h] = summed[k * rows:(k + 1) * rows]
+                xbuf[u, t // H, h, where] = summed[k * tall:(k + 1) * tall]
 
             @pl.when(jnp.logical_not(mine))
             def _():
-                pbuf[u, t] = summed[k * rows:(k + 1) * rows]
-                x_copy(t, u).start()
+                pbuf[u, t, where] = summed[k * tall:(k + 1) * tall]
+                x_copy(t, u, part).start()
 
     def place_of(u):
         block = jnp.where(u < Q, own, edge * C + c)
         return block // blocks, block % blocks, u % Q
 
-    def result_copy(t, u):
+    def result_copy(t, u, part=None):
         home, slot, q = place_of(u)
+        where = span_of(part)
         return pltpu.make_async_remote_copy(
-            src_ref=obuf.at[u, t // H],
-            dst_ref=retbuf.at[slot, q],
-            send_sem=ret_send.at[u, t // H],
+            src_ref=obuf.at[u, t // H, where],
+            dst_ref=retbuf.at[slot, q, where],
+            send_sem=ret_send.at[u],
             recv_sem=ret_recv.at[slot, q],
             device_id={"seq": t // C, "sub": t % C, "heads": home},
             device_id_type=MESH,
@@ -381,35 +453,38 @@
         return pltpu.make_async_remote_copy(
             src_ref=obuf.at[u, t // H],
             dst_ref=mbuf.at[u % Q, t // H],
-            send_sem=ret_send.at[u, t // H],
+            send_sem=ret_send.at[u],
             recv_sem=m_recv.at[u % Q, t // H],
             device_id={"seq": hub_of_edge},
             device_id_type=MESH,
         )
 
-    def reduce(zb, u):
+    def reduce(zb, u, part=None):
         home, slot, q = place_of(u)
+        where = span_of(part)
         for k in range(C):
             t = zb * C + k
 
             @pl.when(t % H == h)
             def _():
-                value = jnp.zeros((rows, thin), jnp.float32)
+                value = jnp.zeros((where.stop - where.start, thin), jnp.float32)
                 for other in range(H):
                     @pl.when(other != h)
                     def _():
                         pltpu.make_async_remote_copy(
-                            src_ref=pbuf.at[u, t], dst_ref=xbuf.at[u, t // H, other],
-                            send_sem=x_send.at[u, t], recv_sem=x_recv.at[u, t // H, other],
+                            src_ref=pbuf.at[u, t, where], dst_ref=xbuf.at[u, t // H, other, where],
+                            send_sem=x_send.at[u], recv_sem=x_recv.at[u, x_slot(t, part), jnp.minimum((other - h - 1) % H, max(H - 2, 0))],
                             device_id={"heads": (h + 1) % H}, device_id_type=MESH,
                         ).wait_recv()
-                    value = value + xbuf[u, t // H, other].astype(jnp.float32)
-                obuf[u, t // H] = value.astype(jnp.bfloat16)
+                    value = value + xbuf[u, t // H, other, where].astype(jnp.float32)
+                obuf[u, t // H, where] = value.astype(jnp.bfloat16)
                 if hub and near:
                     @pl.when(u >= Q)
                     def _():
-                        merge_copy(t, u).wait_recv()
-                        obuf[u, t // H] = (value + mbuf[q, t // H].astype(jnp.float32)).astype(jnp.bfloat16)
+                        if not part:
+                            merge_copy(t, u).wait_recv()
+                        both = value + mbuf[q, t // H, where].astype(jnp.float32)
+                        obuf[u, t // H, where] = both.astype(jnp.bfloat16)
 
                     @pl.when(outer)
                     def _():
@@ -418,59 +493,55 @@
 
                 @pl.when(inner & here)
                 def _():
-                    retbuf[slot, q] = obuf[u, t // H]
+                    retbuf[slot, q, where] = obuf[u, t // H, where]
 
                 @pl.when(inner & jnp.logical_not(here))
                 def _():
-                    result_copy(t, u).start()
-
-    def arrive(zb, e0, e1):
+                    result_copy(t, u, part).start()
+
+    def arrive(zb, parts):
         with jax.named_scope("arrive"):
-            loop(e0, e1, lambda e: from_partner(attbuf, at_send, at_recv, zb, e))
+            for part in parts:
+                landed(zb, part, G - near + (0 if part else near * R))
+
+    def multiply_inner(zb, part=None):
+        with jax.named_scope("mult"):
+            loop(0, Q, lambda u: multiply(zb, u, wall, 0, G, 0, part))
+
+    def multiply_end(zb):
+        with jax.named_scope("arrive"):
+            landed(zb, 0, near * R)
+        with jax.named_scope("multend"):
+            loop(0, Q, lambda u: multiply(zb, u, wall, 0, near, 0))
 
     def multiply_all(zb):
         @pl.when(inner)
         def _():
-            arrive(zb, 0, E)
-            with jax.named_scope("mult"):
-                loop(0, Q, lambda u: multiply(zb, u, wall, 0, G, 0))
+            arrive(zb, range(R))
+            multiply_inner(zb)
 
         if hub and near:
             @pl.when(outer)
             def _():
-                arrive(zb, 0, near * R)
-                with jax.named_scope("multend"):
-                    loop(0, Q, lambda u: multiply(zb, u, wall, 0, near, 0))
-
-    def multiply_extra(zb):
+                multiply_end(zb)
+
+    def multiply_extra(zb, u0=Q, u1=Q + 1, part=None):
         @pl.when(is_hub)
         def _():
             with jax.named_scope("extra"):
-                loop(Q, 2 * Q, lambda u: multiply(zb, u, wext, near, G, near))
-
-    def multiply_most(zb):
-        arrive(zb, 0, (G - 1) * R)
-        with jax.named_scope("most"):
-            loop(0, Q, lambda u: multiply_part(zb, u, wall, 0, G - 1, 0))
-            loop(Q, 2 * Q, lambda u: multiply_part(zb, u, wext, near, G - 1, near))
-
-    def multiply_last(zb):
-        arrive(zb, (G - 1) * R, E)
-        with jax.named_scope("last"):
-            loop(0, Q, lambda u: multiply(zb, u, wall, G - 1, G, 0, True))
-            loop(Q, 2 * Q, lambda u: multiply(zb, u, wext, G - 1, G, near, True))
-
-    def reduce_extra(zb):
+                loop(u0, u1, lambda u: multiply(zb, u, wext, near, G, near, part))
+
+    def reduce_extra(zb, part=None):
         @pl.when(is_hub)
         def _():
             with jax.named_scope("reduceextra"):
-                loop(Q, 2 * Q, lambda u: reduce(zb, u))
-
-    def reduce_all(zb):
+                loop(Q, 2 * Q, lambda u: reduce(zb, u, part))
+
+    def reduce_all(zb, part=None):
         with jax.named_scope("reduce"):
             @pl.when((inner | outer) if near else inner)
             def _():
-                loop(0, Q, lambda u: reduce(zb, u))
+                loop(0, Q, lambda u: reduce(zb, u, part))
 
     def by_slot(k, act, self_slot):
         def pick(which):
@@ -501,6 +572,9 @@
     loop(0, S - 1, wave)
     q_copy.wait()
 
+    def send_rows(e):
+        launch(attbuf, at_send, at_recv, e, *reach(e), by_rows=True)
+
     def att_copy(g):
         return pltpu.make_async_copy(
             attbuf.at[own, g], att_hbm.at[:, pl.ds(pl.multiple_of(g * width, width), width)], out_sem.at[2 + g]
@@ -510,11 +584,23 @@
         with jax.named_scope("attention"):
             attention(g)
         att_copy(g).start()
-        loop(g * R, (g + 1) * R, lambda e: launch(attbuf, at_send, at_recv, e, *reach(e), None, (False, True)))
+        @pl.when(inner)
+        def _():
+            loop(g * R, (g + 1) * R, lambda e: launch(attbuf, at_send, at_recv, e, *reach(e), None, (False, True)))
+
+        if hub:
+            @pl.when(outer)
+            def _():
+                first = jnp.where(g < near, g * R, near * (R - 1) + g)
+                loop(first, first + jnp.where(g < near, R, 1), send_rows)
+
+            @pl.when(outer & (g == 0))
+            def _():
+                loop(NJ, NJ + mid, lambda i: w_out(i).start())
 
         if hub:
             for k in range(2):
-                @pl.when(is_hub & (g < G - 1) & (g * 2 + 1 + k < pieces))
+                @pl.when(is_hub & (g < G - 1) & (g * 2 + 1 + k < NJ))
                 def _():
                     w_relay(g * 2 + 1 + k)
 
@@ -524,6 +610,12 @@
             w_relay(0)
 
     loop(0, G, head_step)
+    if hub:
+        @pl.when(outer)
+        def _():
+            loop(near * (R - 1) + G, E, send_rows)
+            loop(NJ + mid, pieces, lambda i: w_out(i).start())
+
     each_own_weights(lambda copy: copy.wait())
 
     far = jnp.where(z < S // 2, S - 1 - z, z)
@@ -532,7 +624,18 @@
         if hub:
             @pl.when(is_hub & (k == min(1, side_lag)))
             def _():
-                loop(min(pieces, 2 * G - 1), pieces, w_relay)
+                loop(min(NJ, 2 * G - 1), NJ, w_relay)
+
+            @pl.when(is_hub & (k == min(4, E - 1)))
+            def _():
+                loop(NJ, NJ + mid, w_relay)
+
+        last_slot = far * E - 1
+        late, first_late = E + side_lag + 1, NJ + mid
+        if hub and Q > 1:
+            @pl.when(is_hub & (k >= late) & (k < last_slot) & (k - late + first_late < pieces))
+            def _():
+                w_relay(k - late + first_late)
 
         with jax.named_scope("arelay"):
             for rightward in (False, True):
@@ -549,16 +652,18 @@
             @pl.when(is_hub & (k == extra_slot))
             def _():
                 with jax.named_scope("wother"):
-                    for t in range(1, Y):
-                        loop(0, pieces, lambda i: w_pass(i, 1, (y + t) % Y).wait_recv())
-
-        split = hub and G > 1
-        last_slot = far * E - 1
-
-        def unsplit(act):
+                    w_landed(0)
+
+        far_plane = z + inward * far
+
+        def unsplit(act, also=None):
             def guarded(zb):
-                if split:
-                    @pl.when(jnp.logical_not(is_hub & (k == last_slot) & (zb == z + inward * far)))
+                if hub:
+                    skip = is_hub & (zb == far_plane)
+                    if also is not None:
+                        skip = skip | also(zb)
+
+                    @pl.when(jnp.logical_not(skip))
                     def _():
                         act(zb)
                 else:
@@ -569,103 +674,103 @@
         by_slot(k, unsplit(multiply_all), 0)
         if hub:
             by_slot(k, unsplit(multiply_extra), extra_slot)
-        if split:
-            @pl.when(is_hub & (k == last_slot - R))
-            def _():
-                multiply_most(z + inward * far)
-
-            @pl.when(is_hub & (k == last_slot))
-            def _():
-                multiply_last(z + inward * far)
-
-        def reduce_soon(zb):
-            @pl.when(jnp.logical_not(is_hub & (zb == z + inward)))
-            def _():
-                reduce_all(zb)
+            if Q > 1:
+                @pl.when(is_hub & (k == last_slot - 1))
+                def _():
+                    loop(jnp.clip(first_late + last_slot - late, first_late, pieces), pieces, w_relay)
+                    with jax.named_scope("wother2"):
+                        loop(1, Q, w_landed)
+                    for way in (0, 1, -1):
+                        multiply_extra(z + inward * way, Q + 1, 2 * Q)
+                    for part in range(R - 1):
+                        multiply_extra(far_plane, Q + 1, 2 * Q, part)
+            start = (far - 1) * E + near * R
+            for part in range(R):
+                @pl.when(is_hub & (k == start + (part + 1) * (G - near) - 1))
+                def _():
+                    arrive(far_plane, [part])
+                    multiply_inner(far_plane, part)
+                    multiply_extra(far_plane, part=part)
+                    if Q > 1 and part == R - 1:
+                        multiply_extra(far_plane, Q + 1, 2 * Q, part)
 
         @pl.when(k > 1)
         def _():
-            by_slot(k - 2, reduce_soon if hub else reduce_all, self_done)
+            by_slot(k - 2, unsplit(reduce_all, lambda zb: is_hub & (zb == z + inward)), self_done)
 
         if hub:
             @pl.when(is_hub & (k == E + side_lag))
             def _():
                 reduce_all(z + inward)
 
+
     slots = jnp.maximum(far * E, (S - 1 - far) * E + side_lag)
     loop(0, slots, slot_step)
+    def settle(zb):
+        @pl.when(jnp.logical_not((is_hub & (zb == z + inward)) | (is_hub & (zb == z + inward * far))) if hub else True)
+        def _():
+            reduce_all(zb)
+
+    loop(slots - 2, slots, lambda k: by_slot(k, settle, self_done))
     if hub:
         reduce_extra(z)
         reduce_extra(z + inward)
         reduce_extra(z - inward)
-    loop(slots - 2, slots, lambda k: by_slot(k, reduce_all, self_done))
-    if hub:
-        def reduce_far(d):
-            for way in (-inward, inward):
-                zb = z + way * d
-
-                @pl.when((zb >= 0) & (zb < S))
-                def _():
-                    reduce_extra(jnp.clip(zb, 0, S - 1))
-
-        loop(2, S - 1, reduce_far)
-
-    def finish(i):
-        zs, g = i // G, i % G
-        drain(kvbuf, kv_send, kv_recv, zs, g, 0, S - 1)
-
-    def finish_att(i):
-        zs, e = i // E, i % E
-        drain(attbuf, at_send, at_recv, zs, e, *reach(e))
+
+        @pl.when(is_hub)
+        def _():
+            loop(2, far, lambda d: reduce_extra(z + inward * d))
+            for part in range(R):
+                reduce_all(z + inward * far, part)
+                reduce_extra(z + inward * far, part)
 
     with jax.named_scope("drain"):
-        loop(0, S * G, finish)
-        loop(0, S * E, finish_att)
-
-    def each_result(u, act):
-        def one(s):
-            act(s * H + h, u)
-
-        loop(0, n // H, one)
+        loop(0, S, lambda zs: drain(kvbuf, kv_send, zs, None))
+        loop(0, S, lambda zs: drain(attbuf, at_send, zs, near if hub else None))
+
+    units = Q * (2 if hub else 1)
+    partial = n - n // H
+
+    def working(u):
+        return inner & ((u < Q) | is_hub)
 
     def finish_x(u):
-        def finish_one(t):
-            @pl.when(t % H != h)
-            def _():
-                x_copy(t, u).wait_send()
-
-        @pl.when(((u < Q) & ((inner | outer) if near else inner)) | ((u >= Q) & is_hub))
-        def _():
-            loop(0, n, finish_one)
-            if hub and near:
-                @pl.when(outer)
-                def _():
-                    each_result(u, lambda t, u: merge_copy(t, u).wait_send())
+        @pl.when((working(u) | (outer & (u < Q))) if near else working(u))
+        def _():
+            if partial:
+                sized(pbuf.at[u, pl.ds(0, partial)], x_send.at[u], x_send.at[u]).wait_send()
+
+        if hub and near:
+            @pl.when(outer & (u < Q))
+            def _():
+                sized(obuf.at[u], ret_send.at[u], ret_send.at[u]).wait_send()
 
     def finish_results(u):
         home, slot, q = place_of(u)
-
-        def finish_one(t, u):
-            @pl.when(jnp.logical_not((t == own) & (home == h)))
-            def _():
-                result_copy(t, u).wait_send()
-
-        @pl.when(inner & ((u < Q) | is_hub))
-        def _():
-            each_result(u, finish_one)
-
-    units = Q * (2 if hub else 1)
+        kept = (own % H == h) & (home == h)
+
+        @pl.when(working(u) & jnp.logical_not(kept))
+        def _():
+            sized(obuf.at[u], ret_send.at[u], ret_send.at[u]).wait_send()
+
+        if n // H > 1:
+            @pl.when(working(u) & kept)
+            def _():
+                sized(obuf.at[u, pl.ds(0, n // H - 1)], ret_send.at[u], ret_send.at[u]).wait_send()
+
     loop(0, units, finish_x)
 
     if hub:
+        share_rows = wext.at[:, pl.ds(0, part_rows), :]
+
         @pl.when(outer)
         def _():
-            loop(0, pieces, lambda i: w_out(i).wait_send())
+            sized(share_rows, w_send.at[0], w_send.at[0]).wait_send()
 
         @pl.when(is_hub)
         def _():
             for k in range(1, Y):
-                loop(0, pieces, lambda i: w_pass(i, k, y).wait_send())
+                sized(share_rows, wf_send.at[k - 1], wf_send.at[k - 1]).wait_send()
     loop(0, G, lambda g: att_copy(g).wait())
 
     res_copy.wait()
@@ -682,7 +787,7 @@
                 with jax.named_scope(f"final{b}_{q}"):
                     pltpu.make_async_remote_copy(
                         src_ref=obuf.at[0, 0], dst_ref=retbuf.at[b, q],
-                        send_sem=ret_send.at[0, 0], recv_sem=ret_recv.at[b, q],
+                        send_sem=ret_send.at[0], recv_sem=ret_recv.at[b, q],
                         device_id={"heads": (h + 1) % H}, device_id_type=MESH,
                     ).wait_recv()
             where = slice((b * Q + q) * thin, (b * Q + q + 1) * thin)
@@ -706,13 +811,16 @@
         share(k, 0).start()
     hidden_copy.start()
     gain_copy.wait()
-    loop(0, units, finish_results)
+    with jax.named_scope("finres"):
+        loop(0, units, finish_results)
     with jax.named_scope("energy"):
         for k in range(1, H):
             share(k, 1).wait_recv()
     energy = ebuf[0]
     for k in range(1, H):
         energy = energy + ebuf[k]
+    with jax.named_scope("t_normed"):
+        pass
     inverse = lax.rsqrt(energy[:, 0:1] / (H * res_ref.shape[1]) + 1e-06)
     for b in range(blocks):
         where = slice(b * Q * thin, (b + 1) * Q * thin)
@@ -723,8 +831,9 @@
     normed_copy.start()
     for k in range(1, H):
         share(k, 0).wait_send()
-    hidden_copy.wait()
-    normed_copy.wait()
+    with jax.named_scope("outwait"):
+        hidden_copy.wait()
+        normed_copy.wait()
 
 
 def deliver(*refs):
@@ -755,7 +864,8 @@
     near = G // 2
     thin = cols // Q
     U = Q * (2 if hub else 1)
-    E = G * (2 if width // HEAD_WIDTH % 4 == 0 else 1)
+    R = 2 if width // HEAD_WIDTH % 4 == 0 else 1
+    E = G * R
     hbm = pl.BlockSpec(memory_space=pltpu.HBM)
     vmem = pl.BlockSpec(memory_space=pltpu.VMEM)
     dma = pltpu.SemaphoreType.DMA
@@ -774,7 +884,6 @@
             pltpu.SMEM(frame_lengths.shape, jnp.int32),
             pltpu.VMEM(residual_in.shape, bf16),
             pltpu.VMEM(residual_in.shape, bf16),
-            pltpu.VMEM((U, C * rows, thin), f32),
             pltpu.VMEM((n, G, 2, rows, HEAD_WIDTH), bf16),
             pltpu.VMEM((n, G, rows, width), bf16),
             pltpu.VMEM((Q, deep, thin), bf16),
@@ -792,18 +901,20 @@
             dma((5 + Q,)),
             dma((2 + G,)),
             dma((G, 2)),
-            dma((3, S, G)),
-            dma((n, G)),
-            dma((3, S, E)),
-            dma((n, E)),
-            dma((U, n)),
-            dma((U, n // H, H)),
-            dma((U, n // H)),
+            dma((3, S)),
+            dma((S + 1, G)),
+            dma((3, S)),
+            dma((S, E)),
+            dma((S, R)),
+            dma((U,)),
+            dma((U, n // H + (R - 1) * max(1, C // H), max(H - 1, 1))),
+            dma((U,)),
             dma((n // H, Q)),
             dma((Q, n // H)),
+            dma((1,)),
             dma((Q * NJ,)),
-            dma((Y, Q * NJ)),
-            dma((max(Y - 1, 1), Q * NJ)),
+            dma((max(Y - 1, 1), Q)),
+            dma((max(Y - 1, 1),)),
             dma((H,)),
             dma((H,)),
         ],

time: 94.7 us -> 92.3 us (0.975)
  Pallas kernels: 93.9 us -> 91.5 us
    pallas_call x1, Pallas kernels: 91.3 us -> 88.9 us  [shards(): pl.pallas_call(functools.partial(kernel, (S, C, H, G, Y, Q, NJ, hub, near...]
where the time goes in v3:
time: 92.3 us; the launch traced here: 92.1 us
  Pallas kernels  91.5 us (99%)
    pallas_call x1, Pallas kernels, shards(): pl.pallas_call(functools.partial(kernel, (S, C, H, G, Y, Q, NJ, hub, near...  88.9 us
    pallas_call x1, Pallas kernels, shards(): pl.pallas_call(deliver, out_shape=tuple((jax.ShapeDtypeStruct(a.shape, bf...  2.59 us

profile of v3, /device:TPU:0, one launch (start us, length us, event | category | flops | bytes accessed | tf_op | source)
XLA Modules:
  0.0 92.1 jit_solution(3938984205338379048)
XLA Ops:
  0.6 88.9 %shard_map.103 = (bf16[128,4096]{1,0:T(8,128)(2,1)}, bf16[128,2048]{1,0:T(8,128)(2,1)}, bf16[128,2048]{1,0:T(8,128)(2,1)}) custom-call(s32[16]{0:T(128)} %order_hbm.1, s32[8]{0:T(128)} %frames_hbm.1, bf16[128,4096]{1,0:T(8,128)(2,1)} %q_hbm.1, bf16[128,512]{1,0:T(8,128)(2,1)} %k_hbm.1, bf16[128,512]{1,0:T(8,128)(2,1)} %v_hbm.1, bf16[4096,512]{1,0:T(8,128)(2,1)} %proj_hbm.1, ...), custom_call_target="tpu_custom_call" | custom-call | tf_op jit(solution)/shard_map/pallas_call | solution.py:873
  89.5 2.6 %shard_map.104 = (bf16[128,4096]{1,0:T(8,128)(2,1)}, bf16[128,2048]{1,0:T(8,128)(2,1)}, bf16[128,2048]{1,0:T(8,128)(2,1)}) custom-call(bf16[128,4096]{1,0:T(8,128)(2,1)} %get-tuple-element.6.refs_0_, bf16[128,2048]{1,0:T(8,128)(2,1)} %get-tuple-element.7.refs_1_, bf16[128,2048]{1,0:T(8,128)(2,1)} %get-tuple-element.8.refs_2_), custom_call_target="tpu_custom_call" | custom-call | tf_op jit(solution)/shard_map/pallas_call | solution.py:925

commit v4 on v3

--- a/solution.py
+++ b/solution.py
@@ -43,7 +43,7 @@
     R = 2 if steps % 2 == 0 else 1
     E = G * R
     cut_width = width // R
-    side_lag = min(2, E - 1)
+    side_lag = min(5, E - 1)
     mid = min(2, pieces - NJ)
     self_done = E // 2
     extra_slot = min(side_lag + 4, E - 1)
@@ -531,11 +531,11 @@
             with jax.named_scope("extra"):
                 loop(u0, u1, lambda u: multiply(zb, u, wext, near, G, near, part))
 
-    def reduce_extra(zb, part=None):
+    def reduce_extra(zb, part=None, q0=0, q1=Q):
         @pl.when(is_hub)
         def _():
             with jax.named_scope("reduceextra"):
-                loop(Q, 2 * Q, lambda u: reduce(zb, u, part))
+                loop(Q + q0, Q + q1, lambda u: reduce(zb, u, part))
 
     def reduce_all(zb, part=None):
         with jax.named_scope("reduce"):
@@ -631,11 +631,18 @@
                 loop(NJ, NJ + mid, w_relay)
 
         last_slot = far * E - 1
-        late, first_late = E + side_lag + 1, NJ + mid
+        late, first_late = E + side_lag, NJ + mid
         if hub and Q > 1:
             @pl.when(is_hub & (k >= late) & (k < last_slot) & (k - late + first_late < pieces))
             def _():
                 w_relay(k - late + first_late)
+
+        if hub:
+            @pl.when(is_hub & (k == last_slot))
+            def _():
+                for part in range(R - 1):
+                    reduce_all(z + inward * far, part)
+                reduce_extra(z - inward, None, 0, 1)
 
         with jax.named_scope("arelay"):
             for rightward in (False, True):
@@ -675,15 +682,9 @@
         if hub:
             by_slot(k, unsplit(multiply_extra), extra_slot)
             if Q > 1:
-                @pl.when(is_hub & (k == last_slot - 1))
+                @pl.when(is_hub & (k == last_slot))
                 def _():
                     loop(jnp.clip(first_late + last_slot - late, first_late, pieces), pieces, w_relay)
-                    with jax.named_scope("wother2"):
-                        loop(1, Q, w_landed)
-                    for way in (0, 1, -1):
-                        multiply_extra(z + inward * way, Q + 1, 2 * Q)
-                    for part in range(R - 1):
-                        multiply_extra(far_plane, Q + 1, 2 * Q, part)
             start = (far - 1) * E + near * R
             for part in range(R):
                 @pl.when(is_hub & (k == start + (part + 1) * (G - near) - 1))
@@ -692,7 +693,12 @@
                     multiply_inner(far_plane, part)
                     multiply_extra(far_plane, part=part)
                     if Q > 1 and part == R - 1:
-                        multiply_extra(far_plane, Q + 1, 2 * Q, part)
+                        with jax.named_scope("wother2"):
+                            loop(1, Q, w_landed)
+                        for other in range(R):
+                            multiply_extra(far_plane, Q + 1, 2 * Q, other)
+                        for way in (1, -1, 0):
+                            multiply_extra(z + inward * way, Q + 1, 2 * Q)
 
         @pl.when(k > 1)
         def _():
@@ -713,16 +719,21 @@
 
     loop(slots - 2, slots, lambda k: by_slot(k, settle, self_done))
     if hub:
-        reduce_extra(z)
-        reduce_extra(z + inward)
-        reduce_extra(z - inward)
+        last_plane = z + inward * far
 
         @pl.when(is_hub)
         def _():
+            for part in range(R - 1):
+                reduce_extra(last_plane, part, 0, 1)
+            reduce_all(last_plane, R - 1)
+            reduce_extra(last_plane, R - 1, 0, 1)
+            reduce_extra(z + inward, None, 0, 1)
+            reduce_extra(z, None, 0, 1)
+            for part in range(R):
+                reduce_extra(last_plane, part, 1)
+            for way in (1, -1, 0):
+                reduce_extra(z + inward * way, None, 1)
             loop(2, far, lambda d: reduce_extra(z + inward * d))
-            for part in range(R):
-                reduce_all(z + inward * far, part)
-                reduce_extra(z + inward * far, part)
 
     with jax.named_scope("drain"):
         loop(0, S, lambda zs: drain(kvbuf, kv_send, zs, None))
@@ -775,7 +786,9 @@
 
     res_copy.wait()
     squares = jnp.zeros((rows, 1), jnp.float32)
-    for b in range(blocks):
+    shift = jnp.where(h < H // 2, blocks // 2, 0)
+    for i in range(blocks):
+        b = (i + shift) % blocks
         block = h * blocks + b
         source = block // C
         if hub:
@@ -784,19 +797,15 @@
         for q in range(Q):
             @pl.when(jnp.logical_not(made_here))
             def _():
-                with jax.named_scope(f"final{b}_{q}"):
-                    pltpu.make_async_remote_copy(
-                        src_ref=obuf.at[0, 0], dst_ref=retbuf.at[b, q],
-                        send_sem=ret_send.at[0], recv_sem=ret_recv.at[b, q],
-                        device_id={"heads": (h + 1) % H}, device_id_type=MESH,
-                    ).wait_recv()
-            where = slice((b * Q + q) * thin, (b * Q + q + 1) * thin)
+                with jax.named_scope(f"final{i}_{q}"):
+                    sized(retbuf.at[b, q], ret_send.at[0], ret_recv.at[b, q]).wait_recv()
+            where = pl.ds(pl.multiple_of((b * Q + q) * thin, thin), thin)
             hidden = (res_ref[:, where].astype(jnp.float32) + retbuf[b, q].astype(jnp.float32)).astype(jnp.bfloat16)
             hidden_out[:, where] = hidden
             wide = hidden.astype(jnp.float32)
             squares = squares + jnp.sum(wide * wide, axis=-1, keepdims=True)
 
-    ebuf[h] = jnp.broadcast_to(squares, (rows, 128))
+    ebuf[h] = jnp.transpose(jnp.broadcast_to(squares, (rows, 128)))[0:8]
     hidden_copy = pltpu.make_async_copy(hidden_out, hidden_hbm, out_sem.at[0])
 
     def share(k, side):
@@ -819,9 +828,8 @@
     energy = ebuf[0]
     for k in range(1, H):
         energy = energy + ebuf[k]
-    with jax.named_scope("t_normed"):
-        pass
-    inverse = lax.rsqrt(energy[:, 0:1] / (H * res_ref.shape[1]) + 1e-06)
+    inverse = lax.rsqrt(energy / (H * res_ref.shape[1]) + 1e-06)
+    inverse = jnp.transpose(jnp.broadcast_to(inverse[0:1], (128, rows)))[:, 0:1]
     for b in range(blocks):
         where = slice(b * Q * thin, (b + 1) * Q * thin)
         normed_out[:, where] = (
@@ -897,7 +905,7 @@
             pltpu.VMEM((U, n // H, rows, thin), bf16),
             pltpu.VMEM((Q, n // H, rows, thin), bf16),
             pltpu.VMEM((n // H, Q, rows, thin), bf16),
-            pltpu.VMEM((H, rows, 128), f32),
+            pltpu.VMEM((H, 8, rows), f32),
             dma((5 + Q,)),
             dma((2 + G,)),
             dma((G, 2)),

time: 92.3 us -> 88.4 us (0.958)
  Pallas kernels: 91.5 us -> 87.6 us
    pallas_call x1, Pallas kernels: 88.9 us -> 85 us  [shards(): pl.pallas_call(functools.partial(kernel, (S, C, H, G, Y, Q, NJ, hub, near...]
where the time goes in v4:
time: 88.4 us; the launch traced here: 88.2 us
  Pallas kernels  87.6 us (99%)
    pallas_call x1, Pallas kernels, shards(): pl.pallas_call(functools.partial(kernel, (S, C, H, G, Y, Q, NJ, hub, near...  85 us
    pallas_call x1, Pallas kernels, shards(): pl.pallas_call(deliver, out_shape=tuple((jax.ShapeDtypeStruct(a.shape, bf...  2.59 us

profile of v4, /device:TPU:0, one launch (start us, length us, event | category | flops | bytes accessed | tf_op | source)
XLA Modules:
  0.0 88.2 jit_solution(13123947205289560415)
XLA Ops:
  0.6 85.0 %shard_map.103 = (bf16[128,4096]{1,0:T(8,128)(2,1)}, bf16[128,2048]{1,0:T(8,128)(2,1)}, bf16[128,2048]{1,0:T(8,128)(2,1)}) custom-call(s32[16]{0:T(128)} %order_hbm.1, s32[8]{0:T(128)} %frames_hbm.1, bf16[128,4096]{1,0:T(8,128)(2,1)} %q_hbm.1, bf16[128,512]{1,0:T(8,128)(2,1)} %k_hbm.1, bf16[128,512]{1,0:T(8,128)(2,1)} %v_hbm.1, bf16[4096,512]{1,0:T(8,128)(2,1)} %proj_hbm.1, ...), custom_call_target="tpu_custom_call" | custom-call | tf_op jit(solution)/shard_map/pallas_call | solution.py:881
  85.7 2.6 %shard_map.104 = (bf16[128,4096]{1,0:T(8,128)(2,1)}, bf16[128,2048]{1,0:T(8,128)(2,1)}, bf16[128,2048]{1,0:T(8,128)(2,1)}) custom-call(bf16[128,4096]{1,0:T(8,128)(2,1)} %get-tuple-element.6.refs_0_, bf16[128,2048]{1,0:T(8,128)(2,1)} %get-tuple-element.7.refs_1_, bf16[128,2048]{1,0:T(8,128)(2,1)} %get-tuple-element.8.refs_2_), custom_call_target="tpu_custom_call" | custom-call | tf_op jit(solution)/shard_map/pallas_call | solution.py:933

commit v5 on v4

--- a/solution.py
+++ b/solution.py
@@ -640,8 +640,7 @@
         if hub:
             @pl.when(is_hub & (k == last_slot))
             def _():
-                for part in range(R - 1):
-                    reduce_all(z + inward * far, part)
+                reduce_all(z - inward)
                 reduce_extra(z - inward, None, 0, 1)
 
         with jax.named_scope("arelay"):
@@ -692,17 +691,20 @@
                     arrive(far_plane, [part])
                     multiply_inner(far_plane, part)
                     multiply_extra(far_plane, part=part)
+                    if part == R - 1:
+                        for other in range(R - 1):
+                            reduce_all(far_plane, other)
                     if Q > 1 and part == R - 1:
                         with jax.named_scope("wother2"):
                             loop(1, Q, w_landed)
                         for other in range(R):
                             multiply_extra(far_plane, Q + 1, 2 * Q, other)
-                        for way in (1, -1, 0):
+                        for way in (-1, 1, 0):
                             multiply_extra(z + inward * way, Q + 1, 2 * Q)
 
         @pl.when(k > 1)
         def _():
-            by_slot(k - 2, unsplit(reduce_all, lambda zb: is_hub & (zb == z + inward)), self_done)
+            by_slot(k - 2, unsplit(reduce_all, lambda zb: is_hub & ((zb == z + inward) | (zb == z - inward))), self_done)
 
         if hub:
             @pl.when(is_hub & (k == E + side_lag))
@@ -713,7 +715,7 @@
     slots = jnp.maximum(far * E, (S - 1 - far) * E + side_lag)
     loop(0, slots, slot_step)
     def settle(zb):
-        @pl.when(jnp.logical_not((is_hub & (zb == z + inward)) | (is_hub & (zb == z + inward * far))) if hub else True)
+        @pl.when(jnp.logical_not(is_hub & ((zb == z + inward) | (zb == z - inward) | (zb == z + inward * far))) if hub else True)
         def _():
             reduce_all(zb)
 
@@ -725,13 +727,13 @@
         def _():
             for part in range(R - 1):
                 reduce_extra(last_plane, part, 0, 1)
+            reduce_extra(z + inward, None, 0, 1)
             reduce_all(last_plane, R - 1)
             reduce_extra(last_plane, R - 1, 0, 1)
-            reduce_extra(z + inward, None, 0, 1)
             reduce_extra(z, None, 0, 1)
             for part in range(R):
                 reduce_extra(last_plane, part, 1)
-            for way in (1, -1, 0):
+            for way in (-1, 1, 0):
                 reduce_extra(z + inward * way, None, 1)
             loop(2, far, lambda d: reduce_extra(z + inward * d))
 
@@ -848,13 +850,22 @@
     count = len(refs) // 3
     given, out, held = refs[:count], refs[count:2 * count], refs[2 * count:3 * count]
     sem = refs[3 * count]
-    fetch = [pltpu.make_async_copy(given[i], held[i], sem.at[0, i]) for i in range(count)]
-    store = [pltpu.make_async_copy(held[i], out[i], sem.at[1, i]) for i in range(count)]
+    pieces = []
+    for i in reversed(range(count)):
+        tall = given[i].shape[0]
+        cuts = 4 if i == 0 and tall % 32 == 0 else 1
+        pieces += [(i, pl.ds(k * (tall // cuts), tall // cuts)) for k in range(cuts)]
+    fetch = [
+        pltpu.make_async_copy(given[i].at[at], held[i].at[at], sem.at[0, p]) for p, (i, at) in enumerate(pieces)
+    ]
+    store = [
+        pltpu.make_async_copy(held[i].at[at], out[i].at[at], sem.at[1, p]) for p, (i, at) in enumerate(pieces)
+    ]
     for copy in fetch:
         copy.start()
-    for i in range(count):
-        fetch[i].wait()
-        store[i].start()
+    for p in range(len(pieces)):
+        fetch[p].wait()
+        store[p].start()
     for copy in store:
         copy.wait()
 
@@ -935,7 +946,7 @@
         out_shape=tuple(jax.ShapeDtypeStruct(a.shape, bf16) for a in made),
         in_specs=[hbm] * 3,
         out_specs=(hbm,) * 3,
-        scratch_shapes=[pltpu.VMEM(a.shape, bf16) for a in made] + [dma((2, 3))],
+        scratch_shapes=[pltpu.VMEM(a.shape, bf16) for a in made] + [dma((2, 6))],
     )(*made)
 
 

time: 88.4 us -> 87.8 us (level)
  no operation moved by 1% of the time
where the time goes in v5:
time: 87.8 us; the launch traced here: 87.7 us
  Pallas kernels  87.1 us (99%)
    pallas_call x1, Pallas kernels, shards(): pl.pallas_call(functools.partial(kernel, (S, C, H, G, Y, Q, NJ, hub, near...  84.6 us
    pallas_call x1, Pallas kernels, shards(): pl.pallas_call(deliver, out_shape=tuple((jax.ShapeDtypeStruct(a.shape, bf...  2.45 us

profile of v5, /device:TPU:0, one launch (start us, length us, event | category | flops | bytes accessed | tf_op | source)
XLA Modules:
  0.0 87.7 jit_solution(13928753499205622484)
XLA Ops:
  0.6 84.6 %shard_map.103 = (bf16[128,4096]{1,0:T(8,128)(2,1)}, bf16[128,2048]{1,0:T(8,128)(2,1)}, bf16[128,2048]{1,0:T(8,128)(2,1)}) custom-call(s32[16]{0:T(128)} %order_hbm.1, s32[8]{0:T(128)} %frames_hbm.1, bf16[128,4096]{1,0:T(8,128)(2,1)} %q_hbm.1, bf16[128,512]{1,0:T(8,128)(2,1)} %k_hbm.1, bf16[128,512]{1,0:T(8,128)(2,1)} %v_hbm.1, bf16[4096,512]{1,0:T(8,128)(2,1)} %proj_hbm.1, ...), custom_call_target="tpu_custom_call" | custom-call | tf_op jit(solution)/shard_map/pallas_call | solution.py:892
  85.2 2.5 %shard_map.104 = (bf16[128,4096]{1,0:T(8,128)(2,1)}, bf16[128,2048]{1,0:T(8,128)(2,1)}, bf16[128,2048]{1,0:T(8,128)(2,1)}) custom-call(bf16[128,4096]{1,0:T(8,128)(2,1)} %get-tuple-element.6.refs_0_, bf16[128,2048]{1,0:T(8,128)(2,1)} %get-tuple-element.7.refs_1_, bf16[128,2048]{1,0:T(8,128)(2,1)} %get-tuple-element.8.refs_2_), custom_call_target="tpu_custom_call" | custom-call | tf_op jit(solution)/shard_map/pallas_call | solution.py:944
